TPU v7x, 512 devices: a whole 4x8x8 slice. The times are simulated.
512 devices in a mesh: dp: 32 (over x, z), patch: 16 (over y, core).
Axes of the slice: x: 4, y: 8, z: 8, core: 2. Of those that a mesh axis runs over, the one named last changes fastest.
Arguments:
- query_rows: bfloat16 [32, 2048, 576], P('dp', 'patch'), may hold values from -6 to 6
- key_rows: bfloat16 [32, 2048, 576], P('dp', 'patch'), may hold values from -6 to 6
- value_rows: bfloat16 [32, 2048, 576], P('dp', 'patch'), may hold values from -6 to 6
- out_weight: bfloat16 [576, 1152], replicated, may hold values from -0.25 to 0.25
- target: bfloat16 [32, 2048, 1152], P('dp', 'patch'), may hold values from -6 to 6
- lengths: int32 [32], P('dp'), may hold values from 256 to 2048
- segments: int32 [32, 2048], P('dp', 'patch'), may hold values from 0 to 7, never falling along the last dimension, each value on 1 to 1024 neighbouring positions
Outputs:
- query_grad: float32 [32, 2048, 576], P('dp', 'patch')
- key_grad: float32 [32, 2048, 576], P('dp', 'patch')
- value_grad: float32 [32, 2048, 576], P('dp', 'patch')
- weight_grad: float32 [576, 1152], P('patch', 'dp')
- loss: float32 [], replicated
All inputs are finite; a program needn't handle non-finite values.
Results may differ from a plain program's by a relative error of at most 0.024.
Values may be sent and summed in bfloat16 or wider, within the bound.
A program may use at most 64 MiB of HBM per device.

v0:
```python
import functools
import math

import jax
import jax.numpy as jnp
from jax import lax
from jax.experimental import pallas as pl
from jax.experimental.pallas import tpu as pltpu
from jax.sharding import PartitionSpec as P

MESH = pl.DeviceIdType.MESH
WIDTH = 1152
HEADS = 8
HEAD_DIM = 72
FEAT = 576
PAIRS = HEADS // 2
PAIR_ROWS = 2 * HEAD_DIM
FEAT_PAD = 640
SPAN = 256
NEG_LARGE = -1e30
F32 = jnp.float32
BF16 = jnp.bfloat16
KEY, VALUE, QUERY, GRAD = range(4)


def nt(left, right):
    return lax.dot_general(left, right, (((1,), (1,)), ((), ())), preferred_element_type=F32)


def nn(left, right):
    return lax.dot_general(left, right, (((1,), (0,)), ((), ())), preferred_element_type=F32)


def tn(left, right):
    return lax.dot_general(left, right, (((0,), (0,)), ((), ())), preferred_element_type=F32)


def span_start(owner, features):
    return pl.multiple_of(jnp.minimum(owner * features // 128 * 128, FEAT_PAD - SPAN), 128)


def kernel(
    members,
    groups,
    len_ref,
    seg_ref,
    q_ref,
    k_ref,
    v_ref,
    w_hbm,
    t_hbm,
    dq_ref,
    dk_ref,
    dv_ref,
    dw_ref,
    sum_ref,
    w_ref,
    t_ref,
    seg_row_ref,
    all_ref,
    seg_own,
    seg_all,
    stat_own,
    stat_all,
    stat_columns,
    bias_ref,
    prob_ref,
    attn_ref,
    dout_ref,
    part_ref,
    w1_ref,
    keep_ref,
    wx_ref,
    w2_ref,
    wz_ref,
    w3_ref,
    fin_ref,
    w4_ref,
    tile_own,
    tile_all,
    sum_own,
    sum_all,
    load_sem,
    send_sem,
    recv_sem,
    seg_send,
    seg_recv,
    stat_send,
    stat_recv,
    tile_send,
    tile_recv,
    sum_send,
    sum_recv,
    s1,
    r1,
    s2,
    r2,
    s3,
    r3,
    s4,
    r4,
):
    rows = q_ref.shape[1]
    total = rows * members
    chips = members // 2
    half = groups // 2
    outer = groups // 2
    mine = outer // 2
    features = dw_ref.shape[0]
    me = lax.axis_index("patch")
    dp = lax.axis_index("dp")
    chip, core = me // 2, me % 2
    step_a, step_b = dp // 2, dp % 2
    partner = chip * 2 + 1 - core

    def patch_peer(shift):
        return lax.rem(me + shift, members)

    def dp_peer(shift):
        return lax.rem(dp + shift, groups)

    def far(shift):
        return lax.rem(chip + shift, chips)

    loads = [
        pltpu.make_async_copy(seg_ref, seg_row_ref, load_sem.at[0]),
        pltpu.make_async_copy(k_ref, all_ref.at[KEY, me], load_sem.at[1]),
        pltpu.make_async_copy(v_ref, all_ref.at[VALUE, me], load_sem.at[2]),
        pltpu.make_async_copy(q_ref, all_ref.at[QUERY, me], load_sem.at[3]),
        pltpu.make_async_copy(w_hbm, w_ref, load_sem.at[4]),
        pltpu.make_async_copy(t_hbm, t_ref, load_sem.at[5]),
    ]
    for load in loads:
        load.start()

    barrier = pltpu.get_barrier_semaphore()
    for shift in range(1, members):
        pl.semaphore_signal(barrier, inc=1, device_id=(dp, patch_peer(shift)), device_id_type=MESH)
    for shift in range(1, groups):
        pl.semaphore_signal(barrier, inc=1, device_id=(dp_peer(shift), me), device_id_type=MESH)
    loads[0].wait()
    seg_own[...] = jnp.broadcast_to(seg_row_ref[...], seg_own.shape)
    seg_all[me] = seg_own[...]
    for load in loads[1:4]:
        load.wait()
    pl.semaphore_wait(barrier, members + groups - 2)

    def copy(src, dst, send, recv, device):
        return pltpu.make_async_remote_copy(
            src_ref=src, dst_ref=dst, send_sem=send, recv_sem=recv, device_id=device, device_id_type=MESH
        )

    pending = []

    def start(item):
        item.start()
        pending.append(item)

    def rows_of(pair):
        return pl.ds(PAIR_ROWS * pair, PAIR_ROWS)

    def spread(array, pair):
        src = dst = all_ref.at[array, me, rows_of(pair)]
        recv = recv_sem.at[array, me, pair]
        for shift in range(1, chips):
            start(copy(src, dst, send_sem.at[array, shift, pair], recv, (dp, far(shift) * 2 + core)))
        start(copy(src, dst, send_sem.at[array, 0, pair], recv, (dp, partner)))

    def arrived(array, owner, pair):
        slot = all_ref.at[array, owner, rows_of(pair)]
        copy(slot, slot, send_sem.at[array, 0, pair], recv_sem.at[array, owner, pair], (dp, partner)).wait_recv()

    def relay(array, pair):
        for shift in range(1, chips):
            owner = far(shift) * 2 + core
            arrived(array, owner, pair)
            slot = all_ref.at[array, owner, rows_of(pair)]
            send = send_sem.at[array, chips - 1 + shift, pair]
            start(copy(slot, slot, send, recv_sem.at[array, owner, pair], (dp, partner)))

    def finish(array, pair):
        arrived(array, partner, pair)
        for shift in range(1, chips):
            arrived(array, far(shift) * 2 + 1 - core, pair)

    def small(own, everyone, send, recv):
        for shift in range(1, members):
            start(copy(own, everyone.at[me], send.at[shift], recv.at[me], (dp, patch_peer(shift))))

    def small_wait(own, everyone, send, recv):
        for shift in range(1, members):
            owner = patch_peer(shift)
            copy(own, everyone.at[owner], send.at[shift], recv.at[owner], (dp, owner)).wait_recv()

    small(seg_own, seg_all, seg_send, seg_recv)
    for pair in range(PAIRS):
        spread(KEY, pair)
        spread(VALUE, pair)
    for pair in range(PAIRS):
        spread(QUERY, pair)

    upper = lax.broadcasted_iota(jnp.int32, (PAIR_ROWS, 1), 0) < HEAD_DIM
    masks = [upper.astype(F32).astype(BF16), jnp.logical_not(upper).astype(F32).astype(BF16)]

    def stacked(value):
        return jnp.concatenate([value * masks[0], value * masks[1]], axis=1)

    def merged(value):
        return jnp.concatenate([value[:HEAD_DIM, :rows], value[HEAD_DIM:, rows:]], axis=0)

    def part_of(ref, pair):
        return ref[PAIR_ROWS * pair : PAIR_ROWS * (pair + 1), :]

    def own(array, pair):
        return all_ref[array, me, PAIR_ROWS * pair : PAIR_ROWS * (pair + 1), :]

    def whole(array, pair):
        low = PAIR_ROWS * pair
        return jnp.concatenate([all_ref[array, j, low : low + PAIR_ROWS, :] for j in range(members)], axis=1)

    length = len_ref[0]
    lane_position = lax.broadcasted_iota(jnp.int32, (1, rows), 1)
    own_live = me * rows + lax.broadcasted_iota(jnp.int32, (rows, 1), 0) < length
    own_group = jnp.where(me * rows + lane_position < length, seg_own[0:1], -1).astype(F32)
    small_wait(seg_own, seg_all, seg_send, seg_recv)
    for j in range(members):
        group = jnp.where(j * rows + lane_position < length, seg_all[j][0:1], -1).astype(F32)
        group = jnp.broadcast_to(group, (rows, rows)).T
        bias_ref[j * rows : (j + 1) * rows, :] = jnp.where(group == own_group, 0.0, NEG_LARGE)
    attn_ref[FEAT:, :] = jnp.zeros((FEAT_PAD - FEAT, rows), F32)

    log_scale = math.log2(math.e) / math.sqrt(HEAD_DIM)
    score_scale = 1.0 / math.sqrt(HEAD_DIM)

    def biased(scores):
        bias = bias_ref[...]
        return scores * log_scale + jnp.concatenate([bias, bias], axis=1)

    denoms = []
    for pair in range(PAIRS):
        relay(KEY, pair)
        relay(VALUE, pair)
        finish(KEY, pair)
        scores = biased(tn(whole(KEY, pair), stacked(own(QUERY, pair))))
        row_max = jnp.max(scores, axis=0, keepdims=True)
        probs = jnp.exp2(scores - row_max)
        denom = jnp.sum(probs, axis=0, keepdims=True)
        prob_ref[pair] = probs
        log_norm = row_max + jnp.log2(denom)
        for side in (0, 1):
            head = 2 * pair + side
            stat_own[head : head + 1, :] = log_norm[:, side * rows : (side + 1) * rows]
        denoms.append(denom)
        finish(VALUE, pair)
        accum = nn(whole(VALUE, pair), probs.astype(BF16))
        attn_ref[PAIR_ROWS * pair : PAIR_ROWS * (pair + 1), :] = merged(accum / denom)

    attn = attn_ref[...].T.astype(BF16)
    loads[4].wait()
    loads[5].wait()
    output = nn(attn[:, :FEAT], w_ref[...])
    error = jnp.where(own_live, output - t_ref[...].astype(F32), 0.0)
    dout_ref[...] = (2.0 * error).astype(BF16)

    share = WIDTH // groups
    part = tn(dout_ref[...], attn)
    for block in range(groups):
        part_ref[block] = part[block * share : (block + 1) * share].astype(BF16)
    first = core * half
    other = (1 - core) * half
    stage1 = copy(part_ref.at[pl.ds(other, half)], w1_ref, s1, r1, (dp, partner))
    start(stage1)

    for pair in range(PAIRS):
        grad = nt(part_of(w_ref, pair), dout_ref[...]).astype(BF16)
        all_ref[GRAD, me, PAIR_ROWS * pair : PAIR_ROWS * (pair + 1), :] = grad
        spread(GRAD, pair)
        attn_pair = part_of(attn_ref, pair).astype(BF16).astype(F32)
        product = grad.astype(F32) * attn_pair
        for side in (0, 1):
            head = HEADS + 2 * pair + side
            stat_own[head : head + 1, :] = jnp.sum(
                product[HEAD_DIM * side : HEAD_DIM * (side + 1)], axis=0, keepdims=True
            )
    small(stat_own, stat_all, stat_send, stat_recv)
    stat_all[me] = stat_own[...]
    loss_part = jnp.sum(jnp.sum(error * error, axis=0, keepdims=True), axis=1, keepdims=True)
    tile_own[...] = jnp.broadcast_to(loss_part, tile_own.shape)
    small(tile_own, tile_all, tile_send, tile_recv)

    def query_pass(pair):
        low = HEADS + 2 * pair
        delta = jnp.concatenate([stat_own[low : low + 1, :], stat_own[low + 1 : low + 2, :]], axis=1)
        dprobs = tn(whole(VALUE, pair), stacked(own(GRAD, pair)))
        dscores = prob_ref[pair] * (1.0 / denoms[pair]) * (dprobs - delta)
        value = nn(whole(KEY, pair), dscores.astype(BF16))
        dq_ref[PAIR_ROWS * pair : PAIR_ROWS * (pair + 1), :] = merged(value) * score_scale

    stage1.wait_recv()
    stage2 = []
    for i in range(mine):
        away = 2 * i + 1 - step_b
        wx_ref[i] = (part_ref[first + away].astype(F32) + w1_ref[away].astype(F32)).astype(BF16)
        item = copy(wx_ref.at[i], w2_ref.at[i], s2.at[i], r2.at[i], (step_a * 2 + 1 - step_b, me))
        start(item)
        stage2.append(item)
    for i in range(mine):
        near = 2 * i + step_b
        keep_ref[i] = part_ref[first + near].astype(F32) + w1_ref[near].astype(F32)
    for pair in range(PAIRS):
        relay(QUERY, pair)

    query_pass(0)
    query_pass(1)
    relay(GRAD, 0)
    relay(GRAD, 1)
    small_wait(stat_own, stat_all, stat_send, stat_recv)
    for j in range(members):
        tall = jnp.concatenate([stat_all[j], jnp.zeros((128 - 2 * HEADS, rows), F32)], axis=0)
        stat_columns[j * rows : (j + 1) * rows, :] = tall.T

    def third(i):
        stage2[i].wait_recv()
        wz_ref[i] = (keep_ref[i] + w2_ref[i].astype(F32)).astype(BF16)
        owner = core * mine + i
        item = copy(wz_ref.at[i], w3_ref.at[step_a], s3.at[i], r3.at[step_a], (owner * 2 + step_b, me))

        @pl.when(owner != step_a)
        def _():
            item.start()

        return owner, item

    def key_pass(pair):
        def columns(base):
            low = base + 2 * pair
            return jnp.concatenate(
                [jnp.broadcast_to(stat_columns[:, low + side : low + side + 1], (total, rows)) for side in (0, 1)],
                axis=1,
            )

        finish(QUERY, pair)
        finish(GRAD, pair)
        queries = whole(QUERY, pair)
        grads = whole(GRAD, pair)
        scores = biased(tn(queries, stacked(own(KEY, pair))))
        probs = jnp.exp2(scores - columns(0))
        dv_ref[PAIR_ROWS * pair : PAIR_ROWS * (pair + 1), :] = merged(nn(grads, probs.astype(BF16)))
        dprobs = tn(grads, stacked(own(VALUE, pair)))
        dscores = (probs * (dprobs - columns(HEADS))).astype(BF16)
        dk_ref[PAIR_ROWS * pair : PAIR_ROWS * (pair + 1), :] = merged(nn(queries, dscores)) * score_scale

    stage3 = [third(0)]
    relay(GRAD, 2)
    relay(GRAD, 3)
    query_pass(2)
    stage3 += [third(i) for i in range(1, mine)]
    query_pass(3)

    small_wait(tile_own, tile_all, tile_send, tile_recv)
    tile_all[me] = tile_own[...]
    pack_loss = tile_all[0]
    for j in range(1, members):
        pack_loss = pack_loss + tile_all[j]
    tile_lane = lax.broadcasted_iota(jnp.int32, pack_loss.shape, 1)
    sum_own[...] = jnp.where(tile_lane == 0, pack_loss, length.astype(F32))
    for shift in range(1, groups):
        start(copy(sum_own, sum_all.at[dp], sum_send.at[shift], sum_recv.at[dp], (dp_peer(shift), me)))
    sum_all[dp] = sum_own[...]

    key_pass(0)
    key_pass(1)

    collect = step_a // mine
    is_collector = core == collect
    stage4 = []
    for shift in range(1, members):
        target = patch_peer(shift)
        span = fin_ref.at[:, pl.ds(span_start(target, features), SPAN)]
        stage4.append(copy(span, w4_ref.at[chip], s4.at[shift], r4.at[chip], (dp, target)))

    @pl.when(is_collector)
    def _():
        summed = wz_ref[step_a - core * mine].astype(F32)
        for shift in range(1, outer):
            source = lax.rem(step_a + shift, outer)
            copy(wz_ref.at[0], w3_ref.at[source], s3.at[0], r3.at[source], (source * 2 + step_b, me)).wait_recv()
            summed = summed + w3_ref[source].astype(F32)
        fin_ref[...] = summed.astype(BF16)
        for item in stage4:
            item.start()
        w4_ref[chip] = fin_ref[:, pl.ds(span_start(me, features), SPAN)]

    key_pass(2)
    key_pass(3)

    for shift in range(1, groups):
        source = dp_peer(shift)
        copy(sum_own, sum_all.at[source], sum_send.at[shift], sum_recv.at[source], (source, me)).wait_recv()
    totals = sum_all[0]
    for j in range(1, groups):
        totals = totals + sum_all[j]
    sum_ref[...] = totals

    def fetched(owner):
        copy(w4_ref.at[owner], w4_ref.at[owner], s4.at[0], r4.at[owner], (dp, partner)).wait_recv()

    @pl.when(jnp.logical_not(is_collector))
    def _():
        fetched(chip)

    for shift in range(1, chips):
        fetched(far(shift))
    shape = (features, SPAN)
    start_lane = me * features - span_start(me, features)
    chosen = (
        lax.broadcasted_iota(jnp.int32, shape, 1) == start_lane + lax.broadcasted_iota(jnp.int32, shape, 0)
    ).astype(F32).astype(BF16)
    result = nt(chosen, w4_ref[0])
    for j in range(1, chips):
        result = result + nt(chosen, w4_ref[j])
    dw_ref[...] = result

    for item in pending:
        item.wait_send()
    for owner, item in stage3:

        @pl.when(owner != step_a)
        def _():
            item.wait_send()

    @pl.when(is_collector)
    def _():
        for item in stage4:
            item.wait_send()


def scale_kernel(slots, total, sum_ref, dq_ref, dk_ref, dv_ref, dw_ref, query_ref, key_ref, value_ref, weight_ref, loss_ref):
    count = sum_ref[0:1, 1:2]
    ratio = slots / count
    query_ref[...] = dq_ref[...] * ratio
    key_ref[...] = dk_ref[...] * ratio
    value_ref[...] = dv_ref[...] * ratio
    weight_ref[...] = dw_ref[...] * (ratio / total)
    loss_ref[...] = sum_ref[0:1, 0:1] / (count * WIDTH)


def solution(mesh):
    members, groups = mesh.shape["patch"], mesh.shape["dp"]

    def local(query_rows, key_rows, value_rows, out_weight, target, lengths, segments):
        rows = query_rows.shape[1]
        total = rows * members
        chips = members // 2
        outer = groups // 2
        mine = outer // 2
        share = WIDTH // groups
        vmem = pl.BlockSpec(memory_space=pltpu.VMEM)
        hbm = pl.BlockSpec(memory_space=pltpu.HBM)
        dma = pltpu.SemaphoreType.DMA
        outs = pl.pallas_call(
            functools.partial(kernel, members, groups),
            out_shape=(
                jax.ShapeDtypeStruct((FEAT, rows), F32),
                jax.ShapeDtypeStruct((FEAT, rows), F32),
                jax.ShapeDtypeStruct((FEAT, rows), F32),
                jax.ShapeDtypeStruct((FEAT // members, share), F32),
                jax.ShapeDtypeStruct((8, 128), F32),
            ),
            in_specs=[pl.BlockSpec(memory_space=pltpu.SMEM)] + [hbm] * 6,
            out_specs=(vmem,) * 5,
            scratch_shapes=[
                pltpu.VMEM((FEAT, WIDTH), BF16),
                pltpu.VMEM((rows, WIDTH), BF16),
                pltpu.VMEM((1, rows), jnp.int32),
                pltpu.VMEM((4, members, FEAT, rows), BF16),
                pltpu.VMEM((8, rows), jnp.int32),
                pltpu.VMEM((members, 8, rows), jnp.int32),
                pltpu.VMEM((2 * HEADS, rows), F32),
                pltpu.VMEM((members, 2 * HEADS, rows), F32),
                pltpu.VMEM((total, 128), F32),
                pltpu.VMEM((total, rows), F32),
                pltpu.VMEM((PAIRS, total, 2 * rows), F32),
                pltpu.VMEM((FEAT_PAD, rows), F32),
                pltpu.VMEM((rows, WIDTH), BF16),
                pltpu.VMEM((groups, share, FEAT_PAD), BF16),
                pltpu.VMEM((groups // 2, share, FEAT_PAD), BF16),
                pltpu.VMEM((mine, share, FEAT_PAD), F32),
                pltpu.VMEM((mine, share, FEAT_PAD), BF16),
                pltpu.VMEM((mine, share, FEAT_PAD), BF16),
                pltpu.VMEM((mine, share, FEAT_PAD), BF16),
                pltpu.VMEM((outer, share, FEAT_PAD), BF16),
                pltpu.VMEM((share, FEAT_PAD), BF16),
                pltpu.VMEM((chips, share, SPAN), BF16),
                pltpu.VMEM((8, 128), F32),
                pltpu.VMEM((members, 8, 128), F32),
                pltpu.VMEM((8, 128), F32),
                pltpu.VMEM((groups, 8, 128), F32),
                dma((6,)),
                dma((4, members, PAIRS)),
                dma((4, members, PAIRS)),
                dma((members,)),
                dma((members,)),
                dma((members,)),
                dma((members,)),
                dma((members,)),
                dma((members,)),
                dma((groups,)),
                dma((groups,)),
                dma,
                dma,
                dma((mine,)),
                dma((mine,)),
                dma((mine,)),
                dma((outer,)),
                dma((members,)),
                dma((chips,)),
            ],
            compiler_params=pltpu.CompilerParams(collective_id=0, has_side_effects=True, vmem_limit_bytes=65900000),
            name="sublayer",
        )(
            lengths,
            segments,
            query_rows[0].T,
            key_rows[0].T,
            value_rows[0].T,
            out_weight,
            target[0],
        )
        final = pl.pallas_call(
            functools.partial(scale_kernel, groups * total, total),
            out_shape=(
                jax.ShapeDtypeStruct((FEAT, rows), F32),
                jax.ShapeDtypeStruct((FEAT, rows), F32),
                jax.ShapeDtypeStruct((FEAT, rows), F32),
                jax.ShapeDtypeStruct((FEAT // members, share), F32),
                jax.ShapeDtypeStruct((1, 1), F32),
            ),
            in_specs=[vmem] * 5,
            out_specs=(vmem,) * 5,
            compiler_params=pltpu.CompilerParams(vmem_limit_bytes=65900000),
            name="scale",
        )(outs[4], *outs[:4])
        return (final[0].T[None], final[1].T[None], final[2].T[None], final[3], final[4].reshape(()))

    placed = (
        P("dp", "patch", None),
        P("dp", "patch", None),
        P("dp", "patch", None),
        P(),
        P("dp", "patch", None),
        P("dp"),
        P("dp", "patch"),
    )
    return jax.shard_map(
        local,
        mesh=mesh,
        in_specs=placed,
        out_specs=(
            P("dp", "patch", None),
            P("dp", "patch", None),
            P("dp", "patch", None),
            P("patch", "dp"),
            P(),
        ),
        check_vma=False,
    )
```

profile of v0, /device:TPU:1, one launch (start us, length us, event | category | flops | bytes accessed | tf_op | source)
XLA Modules:
  0.0 153.5 jit_solution(2651979363481117171)
XLA Ops:
  1.3 150.0 %sublayer.1 = (f32[576,128]{1,0:T(8,128)}, f32[576,128]{1,0:T(8,128)}, f32[576,128]{1,0:T(8,128)}, f32[36,36]{1,0:T(8,128)}, f32[8,128]{1,0:T(8,128)}) custom-call(s32[1]{0:T(128)S(6)} %copy.12.len_ref, s32[1,128]{1,0:T(1,128)} %seg_ref.1, bf16[576,128]{1,0:T(8,128)(2,1)} %bitcast.21, bf16[576,128]{1,0:T(8,128)(2,1)} %bitcast.22, bf16[576,128]{1,0:T(8,128)(2,1)} %bitcast.23, ...), custom_call_target="tpu_custom_call" | custom-call | tf_op jit(solution)/shard_map/sublayer/pallas_call | solution.py:461
  151.3 2.2 %scale.1 = (f32[576,128]{1,0:T(8,128)}, f32[576,128]{1,0:T(8,128)}, f32[576,128]{1,0:T(8,128)}, f32[36,36]{1,0:T(8,128)}, f32[1,1]{1,0:T(1,128)}) custom-call(f32[8,128]{1,0:T(8,128)} %get-tuple-element.15.sum_ref, f32[576,128]{1,0:T(8,128)} %get-tuple-element.16.dq_ref, f32[576,128]{1,0:T(8,128)} %get-tuple-element.17.dk_ref, ...), custom_call_target="tpu_custom_call" | custom-call | tf_op jit(solution)/shard_map/scale/pallas_call | solution.py:530
where the time goes:
time: 156 us; the launch traced here: 153 us
  Pallas kernels  152 us (97%)
    pallas_call x1, Pallas kernels, local(): pl.pallas_call(functools.partial(kernel, members, groups), out_shape=(jax...  150 us

commit v1 on v0

v1 whole, which is shorter than its diff:
```python
import functools
import math

import jax
import jax.numpy as jnp
from jax import lax
from jax.experimental import pallas as pl
from jax.experimental.pallas import tpu as pltpu
from jax.sharding import PartitionSpec as P

MESH = pl.DeviceIdType.MESH
WIDTH = 1152
HEADS = 8
HEAD_DIM = 72
FEAT = 576
FEAT_PAD = 640
FM = 80
LANES = 128
SPAN = 256
TILE = 256
CHUNK = 512
NEG_LARGE = -1e30
F32 = jnp.float32
BF16 = jnp.bfloat16
XS, ZS = 4, 8
ZH = ZS // 2


def nt(left, right):
    return lax.dot_general(left, right, (((1,), (1,)), ((), ())), preferred_element_type=F32)


def nn(left, right):
    return lax.dot_general(left, right, (((1,), (0,)), ((), ())), preferred_element_type=F32)


def tn(left, right):
    return lax.dot_general(left, right, (((0,), (0,)), ((), ())), preferred_element_type=F32)


def span_start(owner, features):
    return pl.multiple_of(jnp.minimum(owner * features // 128 * 128, FEAT_PAD - SPAN), 128)


def kernel(
    members,
    groups,
    len_ref,
    seg_ref,
    q_ref,
    k_ref,
    v_ref,
    w_hbm,
    t_hbm,
    dq_ref,
    dk_ref,
    dv_ref,
    dw_ref,
    sum_ref,
    q_in,
    k_in,
    v_in,
    w_ref,
    t_ref,
    seg_row,
    seg_all,
    q_slab,
    k_slab,
    v_slab,
    k_tm,
    v_tm,
    k_fm,
    v_fm,
    q_fm,
    g_fm,
    qs_fm,
    gs_fm,
    s_ref,
    p_ref,
    ds_ref,
    att_out,
    attn_all,
    attn_tm,
    dout_ref,
    g_out,
    g_slab,
    xv_out,
    xv_in,
    xk_out,
    xk_in,
    v_own,
    k_own,
    oq,
    ok,
    ov,
    part_ref,
    w1_ref,
    sum1_ref,
    keep_ref,
    w2_ref,
    wz_ref,
    w3_ref,
    fin_ref,
    w4_ref,
    tile_own,
    tile_all,
    sum_own,
    sum_all,
    load_sem,
    send_sem,
    seg_recv,
    q_recv,
    k_recv,
    v_recv,
    attn_recv,
    g_recv,
    xv_recv,
    xk_recv,
    dq_recv,
    dk_recv,
    dv_recv,
    tile_recv,
    sum_recv,
    r1,
    r2,
    r3,
    r4,
):
    rows = t_ref.shape[0]
    chips = members // 2
    features = dw_ref.shape[0]
    queries = chips * rows
    me = lax.axis_index("patch")
    dp = lax.axis_index("dp")
    chip, core = me // 2, me % 2
    cx, cz = dp // ZS, dp % ZS
    partner = chip * 2 + 1 - core

    loads = [
        pltpu.make_async_copy(src, dst, load_sem.at[i])
        for i, (src, dst) in enumerate(
            [(seg_ref, seg_row), (k_ref, k_in), (q_ref, q_in), (v_ref, v_in), (w_hbm, w_ref), (t_hbm, t_ref)]
        )
    ]
    for load in loads:
        load.start()

    barrier = pltpu.get_barrier_semaphore()
    for shift in range(1, members):
        pl.semaphore_signal(barrier, inc=1, device_id=(dp, lax.rem(me + shift, members)), device_id_type=MESH)
    for shift in range(1, groups):
        pl.semaphore_signal(barrier, inc=1, device_id=(lax.rem(dp + shift, groups), me), device_id_type=MESH)
    for load in loads[:4]:
        load.wait()
    seg_all[0] = seg_row[...]
    pl.semaphore_wait(barrier, members + groups - 2)

    count = [0]
    pending = []

    def copy(src, dst, recv, device, send=None):
        if send is None:
            send = send_sem.at[count[0]]
            count[0] += 1
        return pltpu.make_async_remote_copy(
            src_ref=src, dst_ref=dst, send_sem=send, recv_sem=recv, device_id=device, device_id_type=MESH
        )

    def start(item):
        item.start()
        pending.append(item)

    def arrived(slot, recv):
        copy(slot, slot, recv, (dp, partner), send=send_sem.at[0]).wait_recv()

    def far(shift):
        return lax.rem(chip + shift, chips)

    def same(shift):
        return (dp, far(shift) * 2 + core)

    def cross(shift):
        return (dp, far(shift) * 2 + 1 - core)

    shifts = list(range(1, chips))
    for s in shifts:
        start(copy(seg_row, seg_all.at[chips - s], seg_recv.at[chips - s], same(s)))
    for s in range(chips):
        slot = chips + (chips - s) % chips
        start(copy(seg_row, seg_all.at[slot], seg_recv.at[slot], cross(s)))
    order = [4, 3, 5, 2, 6, 1, 7]
    start(copy(k_in.at[chip], k_slab.at[chips], k_recv.at[chips], cross(0)))
    start(copy(v_in.at[chip], v_slab.at[chips], v_recv.at[chips], cross(0)))
    for source, slab, recv in ((k_in, k_slab, k_recv), (q_in, q_slab, q_recv), (v_in, v_slab, v_recv)):
        for s in order:
            start(copy(source.at[far(s)], slab.at[chips - s], recv.at[chips - s], same(s)))

    length = len_ref[0]
    lane = lax.broadcasted_iota(jnp.int32, (1, rows), 1)
    sublane = lax.broadcasted_iota(jnp.int32, (16, rows), 0)

    def is_group(slot):
        owner = far(slot % chips) * 2 + (core if slot < chips else 1 - core)
        group = jnp.where(owner * rows + lane < length, seg_all[slot], -1) + 1
        return jnp.broadcast_to(group, (16, rows)) == sublane

    zeros40 = jnp.zeros((40, rows), F32)
    zeros48 = jnp.zeros((48, rows), F32)
    zeros8 = jnp.zeros((8, rows), F32)
    ones8 = jnp.ones((8, rows), F32)

    def columns(slot):
        return slice(slot * rows, (slot + 1) * rows)

    def take_key(slot, value):
        code = jnp.where(is_group(slot), 1.0, 0.0)
        full = jnp.concatenate([value.astype(F32), code, zeros40], axis=0)
        k_fm[:, columns(slot)] = full[:FM].astype(BF16)
        k_tm[columns(slot), :] = full.T.astype(BF16)

    def take_value(slot, value):
        full = jnp.concatenate([value.astype(F32), ones8, zeros48], axis=0)
        v_fm[:, columns(slot)] = full[:FM].astype(BF16)
        v_tm[columns(slot), :] = full.T.astype(BF16)

    def take_query(slot, value):
        code = jnp.where(is_group(slot), 0.0, NEG_LARGE)
        q_fm[:, columns(slot)] = jnp.concatenate([value.astype(F32), code, zeros40], axis=0).astype(BF16)

    for slot in range(1, members):
        arrived(seg_all.at[slot], seg_recv.at[slot])

    take_key(0, k_in[chip])
    for s in order:
        slot = chips - s
        arrived(k_slab.at[slot], k_recv.at[slot])
        start(copy(k_slab.at[slot], k_slab.at[chips + slot], k_recv.at[chips + slot], cross(0)))
        take_key(slot, k_slab[slot])
    for s in [0] + order:
        slot = chips + (chips - s) % chips
        arrived(k_slab.at[slot], k_recv.at[slot])
        take_key(slot, k_slab[slot])
    take_query(0, q_in[chip])
    for s in order:
        slot = chips - s
        arrived(q_slab.at[slot], q_recv.at[slot])
        take_query(slot, q_slab[slot])

    log_scale = math.log2(math.e) / math.sqrt(HEAD_DIM)
    score_scale = 1.0 / math.sqrt(HEAD_DIM)
    total = rows * members
    tiles = queries // TILE
    per_tile = TILE // rows
    chunks = [slice(low, low + CHUNK) for low in range(0, total, CHUNK)]

    def score_tile(t):
        span = slice(t * TILE, (t + 1) * TILE)
        tile = q_fm[:, span]
        top = None
        for chunk in chunks:
            scores = nn(k_tm[chunk, :], tile)
            s_ref[t % 2, chunk, :] = scores
            peak = jnp.max(scores, axis=0, keepdims=True)
            top = peak if top is None else jnp.maximum(top, peak)
        top = top * log_scale
        for chunk in chunks:
            p_ref[chunk, span] = jnp.exp2(s_ref[t % 2, chunk, :] * log_scale - top).astype(BF16)

    tile_order = list(range(1, tiles)) + [0]
    for t in tile_order[:2]:
        score_tile(t)
    take_value(0, v_in[chip])
    for s in order:
        slot = chips - s
        arrived(v_slab.at[slot], v_recv.at[slot])
        start(copy(v_slab.at[slot], v_slab.at[chips + slot], v_recv.at[chips + slot], cross(0)))
        take_value(slot, v_slab[slot])
    for t in tile_order[2:]:
        score_tile(t)
    for s in [0] + order:
        slot = chips + (chips - s) % chips
        arrived(v_slab.at[slot], v_recv.at[slot])
        take_value(slot, v_slab[slot])

    inverse = [None] * chips
    for t in tile_order:
        accum = nn(v_fm[...], p_ref[:, t * TILE : (t + 1) * TILE])
        for i in range(per_tile):
            slot = t * per_tile + i
            denom = accum[HEAD_DIM : HEAD_DIM + 1, i * rows : (i + 1) * rows]
            inverse[slot] = 1.0 / denom
            attn = (accum[:HEAD_DIM, i * rows : (i + 1) * rows] / denom).astype(BF16)
            att_out[slot] = attn
            if slot:
                start(copy(att_out.at[slot], attn_all.at[chip], attn_recv.at[chips - slot], same(slot)))
            else:
                attn_all[chip] = attn
    for slot in range(chips):
        scaled = q_fm[:HEAD_DIM, columns(slot)].astype(F32) * (inverse[slot] * score_scale)
        qs_fm[:, columns(slot)] = jnp.concatenate([scaled, zeros8], axis=0).astype(BF16)

    loads[4].wait()
    loads[5].wait()
    for s in order:
        arrived(attn_all.at[far(s)], attn_recv.at[s])
    stacked = [attn_all[h].astype(F32) for h in range(HEADS)] + [jnp.zeros((FEAT_PAD - FEAT, rows), F32)]
    attn_tm[...] = jnp.concatenate(stacked, axis=0).T.astype(BF16)
    own_live = me * rows + lax.broadcasted_iota(jnp.int32, (rows, 1), 0) < length
    output = nn(attn_tm[:, :FEAT], w_ref[...])
    error = jnp.where(own_live, output - t_ref[...].astype(F32), 0.0)
    dout_ref[...] = (2.0 * error).astype(BF16)
    grad = nt(w_ref[...], dout_ref[...])
    for h in range(HEADS):
        g_out[h] = grad[HEAD_DIM * h : HEAD_DIM * (h + 1)].astype(BF16)
    for s in order:
        start(copy(g_out.at[far(s)], g_slab.at[chips - s], g_recv.at[chips - s], same(s)))

    loss_part = jnp.sum(jnp.sum(error * error, axis=0, keepdims=True), axis=1, keepdims=True)
    tile_own[...] = jnp.broadcast_to(loss_part, tile_own.shape)
    for shift in range(1, members):
        peer = lax.rem(me + shift, members)
        start(copy(tile_own, tile_all.at[members - shift], tile_recv.at[members - shift], (dp, peer)))
    tile_all[0] = tile_own[...]

    share = WIDTH // groups
    part = tn(dout_ref[...], attn_tm[...])
    for block in range(groups):
        x, z = block // ZS, block % ZS
        part_ref[z % 2, x, z // 2] = part[block * share : (block + 1) * share].astype(BF16)
    start(copy(part_ref.at[1 - core], w1_ref, r1, (dp, partner)))

    arrived(w1_ref, r1)
    for x in range(XS):
        for z in range(ZH):
            sum1_ref[x, z] = (part_ref[core, x, z].astype(F32) + w1_ref[x, z].astype(F32)).astype(BF16)
    for d in range(1, XS):
        x = lax.rem(cx + d, XS)
        start(copy(sum1_ref.at[x], w2_ref.at[XS - d - 1], r2.at[XS - d - 1], (x * ZS + cz, me)))
    for z in range(ZH):
        keep_ref[z] = part_ref[core, cx, z].astype(F32) + w1_ref[cx, z].astype(F32)

    def take_grad(slot, value):
        wide = value.astype(F32)
        delta = -jnp.sum(wide * att_out[slot].astype(F32), axis=0, keepdims=True)
        high = delta.astype(BF16).astype(F32)
        middle = (delta - high).astype(BF16).astype(F32)
        low = delta - high - middle
        index = lax.broadcasted_iota(jnp.int32, (8, rows), 0)
        extra = jnp.where(index == 0, high, jnp.where(index == 1, middle, jnp.where(index == 2, low, 0.0)))
        g_fm[:, columns(slot)] = jnp.concatenate([wide, extra, zeros48], axis=0).astype(BF16)
        gs_fm[:, columns(slot)] = jnp.concatenate([wide * inverse[slot], zeros8], axis=0).astype(BF16)

    take_grad(0, g_out[chip])
    for s in order:
        slot = chips - s
        arrived(g_slab.at[slot], g_recv.at[slot])
        take_grad(slot, g_slab[slot])

    def key_side(left, right_ref, mine, out_ref, in_ref, recv):
        for i in list(range(chips, members, 2)) + list(range(0, chips, 2)):
            result = nt(left, right_ref[i * rows : (i + 2) * rows, :])
            target, base = (out_ref, i - chips) if i >= chips else (mine, i)
            for j in range(2):
                target[base + j] = result[:HEAD_DIM, j * rows : (j + 1) * rows]
            if i >= chips:
                pair = pl.ds(base, 2)
                start(copy(out_ref.at[pair], in_ref.at[pair], recv.at[base // 2], (dp, partner)))

    def send_home(slot, out, ref, recv):
        if slot:
            start(copy(out.at[slot], ref.at[chip], recv.at[chips - slot], same(slot)))
        else:
            item = pltpu.make_async_copy(out.at[0], ref.at[chip], send_sem.at[count[0]])
            count[0] += 1
            item.start()
            local.append(item)

    local = []

    def key_home(mine, in_ref, recv, out, ref, home):
        for base in (2, 4, 6, 0):
            pair = in_ref.at[pl.ds(base, 2)]
            arrived(pair, recv.at[base // 2])
            for slot in (base, base + 1):
                out[slot] = (mine[slot] + in_ref[slot]).astype(BF16)
                send_home(slot, out, ref, home)

    key_side(gs_fm[...], p_ref, v_own, xv_out, xv_in, xv_recv)
    key_home(v_own, xv_in, xv_recv, ov, dv_ref, dv_recv)

    for t in tile_order:
        span = slice(t * TILE, (t + 1) * TILE)
        tile = g_fm[:, span]
        for chunk in chunks:
            dprobs = nn(v_tm[chunk, :], tile)
            ds_ref[chunk, span] = (p_ref[chunk, span].astype(F32) * dprobs).astype(BF16)
        dq = nn(k_fm[...], ds_ref[:, span])
        for i in range(per_tile):
            slot = t * per_tile + i
            oq[slot] = (dq[:HEAD_DIM, i * rows : (i + 1) * rows] * (inverse[slot] * score_scale)).astype(BF16)
            send_home(slot, oq, dq_ref, dq_recv)

    key_side(qs_fm[...], ds_ref, k_own, xk_out, xk_in, xk_recv)
    key_home(k_own, xk_in, xk_recv, ok, dk_ref, dk_recv)

    for slot in range(1, members):
        arrived(tile_all.at[slot], tile_recv.at[slot])
    pack_loss = tile_all[0]
    for slot in range(1, members):
        pack_loss = pack_loss + tile_all[slot]
    sum_own[...] = jnp.where(lane == 0, pack_loss, length.astype(F32))
    for shift in range(1, groups):
        peer = lax.rem(dp + shift, groups)
        start(copy(sum_own, sum_all.at[groups - shift], sum_recv.at[groups - shift], (peer, me)))
    sum_all[0] = sum_own[...]

    for d in range(1, XS):
        arrived(w2_ref.at[d - 1], r2.at[d - 1])
    for z in range(ZH):
        summed = keep_ref[z]
        for d in range(XS - 1):
            summed = summed + w2_ref[d, z].astype(F32)
        wz_ref[z] = summed.astype(BF16)
    stage3 = []
    for z in range(ZH):
        target = 2 * z + core
        item = copy(wz_ref.at[z], w3_ref.at[cz], r3.at[cz], (cx * ZS + target, me))
        stage3.append((target, item))

        @pl.when(target != cz)
        def _():
            item.start()

    is_collector = core == cz % 2
    stage4 = []
    for shift in range(1, members):
        target = lax.rem(me + shift, members)
        span = fin_ref.at[:, pl.ds(span_start(target, features), SPAN)]
        stage4.append(copy(span, w4_ref.at[chip], r4.at[chip], (dp, target)))

    @pl.when(is_collector)
    def _():
        summed = wz_ref[cz // 2].astype(F32)
        for shift in range(1, ZS):
            source = lax.rem(cz + shift, ZS)
            arrived(w3_ref.at[source], r3.at[source])
            summed = summed + w3_ref[source].astype(F32)
        fin_ref[...] = summed.astype(BF16)
        for item in stage4:
            item.start()
        w4_ref[chip] = fin_ref[:, pl.ds(span_start(me, features), SPAN)]

    for shift in range(1, groups):
        arrived(sum_all.at[shift], sum_recv.at[shift])
    totals = sum_all[0]
    for shift in range(1, groups):
        totals = totals + sum_all[shift]
    sum_ref[...] = totals

    for s in order:
        for ref, recv in ((dv_ref, dv_recv), (dq_ref, dq_recv), (dk_ref, dk_recv)):
            arrived(ref.at[far(s)], recv.at[s])

    @pl.when(jnp.logical_not(is_collector))
    def _():
        arrived(w4_ref.at[chip], r4.at[chip])

    for s in shifts:
        arrived(w4_ref.at[far(s)], r4.at[far(s)])
    shape = (features, SPAN)
    start_lane = me * features - span_start(me, features)
    chosen = (
        lax.broadcasted_iota(jnp.int32, shape, 1) == start_lane + lax.broadcasted_iota(jnp.int32, shape, 0)
    ).astype(F32).astype(BF16)
    result = nt(chosen, w4_ref[0])
    for j in range(1, chips):
        result = result + nt(chosen, w4_ref[j])
    dw_ref[...] = result

    for item in local:
        item.wait()
    for item in pending:
        item.wait_send()
    for target, item in stage3:

        @pl.when(target != cz)
        def _():
            item.wait_send()

    @pl.when(is_collector)
    def _():
        for item in stage4:
            item.wait_send()


def scale_kernel(slots, total, sum_ref, dq_ref, dk_ref, dv_ref, dw_ref, query_ref, key_ref, value_ref, weight_ref, loss_ref):
    count = sum_ref[0:1, 1:2]
    ratio = slots / count
    for source, target in ((dq_ref, query_ref), (dk_ref, key_ref), (dv_ref, value_ref)):
        for h in range(HEADS):
            target[HEAD_DIM * h : HEAD_DIM * (h + 1), :] = source[h].astype(F32) * ratio
    weight_ref[...] = dw_ref[...] * (ratio / total)
    loss_ref[...] = sum_ref[0:1, 0:1] / (count * WIDTH)


def solution(mesh):
    members, groups = mesh.shape["patch"], mesh.shape["dp"]

    def local(query_rows, key_rows, value_rows, out_weight, target, lengths, segments):
        rows = query_rows.shape[1]
        total = rows * members
        chips = members // 2
        queries = rows * chips
        share = WIDTH // groups
        vmem = pl.BlockSpec(memory_space=pltpu.VMEM)
        hbm = pl.BlockSpec(memory_space=pltpu.HBM)
        dma = pltpu.SemaphoreType.DMA
        slab = (HEAD_DIM, rows)

        def heads(value):
            return value[0].T.reshape(HEADS, HEAD_DIM, rows)

        def bf(*shape):
            return pltpu.VMEM(shape, BF16)

        def fl(*shape):
            return pltpu.VMEM(shape, F32)

        outs = pl.pallas_call(
            functools.partial(kernel, members, groups),
            out_shape=(
                jax.ShapeDtypeStruct((HEADS, HEAD_DIM, rows), BF16),
                jax.ShapeDtypeStruct((HEADS, HEAD_DIM, rows), BF16),
                jax.ShapeDtypeStruct((HEADS, HEAD_DIM, rows), BF16),
                jax.ShapeDtypeStruct((FEAT // members, share), F32),
                jax.ShapeDtypeStruct((1, LANES), F32),
            ),
            in_specs=[pl.BlockSpec(memory_space=pltpu.SMEM)] + [hbm] * 6,
            out_specs=(hbm, hbm, hbm, vmem, vmem),
            scratch_shapes=[
                bf(HEADS, *slab),
                bf(HEADS, *slab),
                bf(HEADS, *slab),
                bf(FEAT, WIDTH),
                bf(rows, WIDTH),
                pltpu.VMEM((1, rows), jnp.int32),
                pltpu.VMEM((members, 1, rows), jnp.int32),
                bf(chips, *slab),
                bf(members, *slab),
                bf(members, *slab),
                bf(total, LANES),
                bf(total, LANES),
                bf(FM, total),
                bf(FM, total),
                bf(LANES, queries),
                bf(LANES, queries),
                bf(FM, queries),
                bf(FM, queries),
                fl(2, total, TILE),
                bf(total, queries),
                bf(total, queries),
                bf(chips, *slab),
                bf(HEADS, *slab),
                bf(rows, FEAT_PAD),
                bf(rows, WIDTH),
                bf(HEADS, *slab),
                bf(chips, *slab),
                fl(chips, *slab),
                fl(chips, *slab),
                fl(chips, *slab),
                fl(chips, *slab),
                fl(chips, *slab),
                fl(chips, *slab),
                bf(chips, *slab),
                bf(chips, *slab),
                bf(chips, *slab),
                bf(2, XS, ZH, share, FEAT_PAD),
                bf(XS, ZH, share, FEAT_PAD),
                bf(XS, ZH, share, FEAT_PAD),
                fl(ZH, share, FEAT_PAD),
                bf(XS - 1, ZH, share, FEAT_PAD),
                bf(ZH, share, FEAT_PAD),
                bf(ZS, share, FEAT_PAD),
                bf(share, FEAT_PAD),
                bf(chips, share, SPAN),
                fl(1, LANES),
                fl(members, 1, LANES),
                fl(1, LANES),
                fl(groups, 1, LANES),
                dma((6,)),
                dma((200,)),
                dma((members,)),
                dma((chips,)),
                dma((members,)),
                dma((members,)),
                dma((chips,)),
                dma((chips,)),
                dma((chips // 2,)),
                dma((chips // 2,)),
                dma((chips,)),
                dma((chips,)),
                dma((chips,)),
                dma((members,)),
                dma((groups,)),
                dma,
                dma((XS - 1,)),
                dma((ZS,)),
                dma((chips,)),
            ],
            compiler_params=pltpu.CompilerParams(collective_id=0, has_side_effects=True, vmem_limit_bytes=65900000),
            name="sublayer",
        )(
            lengths,
            segments,
            heads(query_rows),
            heads(key_rows),
            heads(value_rows),
            out_weight,
            target[0],
        )
        final = pl.pallas_call(
            functools.partial(scale_kernel, groups * total, total),
            out_shape=(
                jax.ShapeDtypeStruct((FEAT, rows), F32),
                jax.ShapeDtypeStruct((FEAT, rows), F32),
                jax.ShapeDtypeStruct((FEAT, rows), F32),
                jax.ShapeDtypeStruct((FEAT // members, share), F32),
                jax.ShapeDtypeStruct((1, 1), F32),
            ),
            in_specs=[vmem] * 5,
            out_specs=(vmem,) * 5,
            compiler_params=pltpu.CompilerParams(vmem_limit_bytes=65900000),
            name="scale",
        )(outs[4], *outs[:4])
        return (final[0].T[None], final[1].T[None], final[2].T[None], final[3], final[4].reshape(()))

    placed = (
        P("dp", "patch", None),
        P("dp", "patch", None),
        P("dp", "patch", None),
        P(),
        P("dp", "patch", None),
        P("dp"),
        P("dp", "patch"),
    )
    return jax.shard_map(
        local,
        mesh=mesh,
        in_specs=placed,
        out_specs=(
            P("dp", "patch", None),
            P("dp", "patch", None),
            P("dp", "patch", None),
            P("patch", "dp"),
            P(),
        ),
        check_vma=False,
    )
```

time: 156 us -> 73.1 us (0.47); the launches traced: 153 us -> 72.9 us
  Pallas kernels: 152 us -> 71.6 us
    pallas_call x1, Pallas kernels: 150 us -> 69.5 us  [local(): pl.pallas_call(functools.partial(kernel, members, groups), out_shape=(jax...]
where the time goes in v1:
time: 73.1 us; the launch traced here: 72.9 us
  Pallas kernels  71.6 us (98%)
  between operations  1.29 us (2%)
    pallas_call x1, Pallas kernels, local(): pl.pallas_call(functools.partial(kernel, members, groups), out_shape=(jax...  69.5 us
    pallas_call x1, Pallas kernels, local(): pl.pallas_call(functools.partial(scale_kernel, groups * total, total), ou...  2.07 us

profile of v1, /device:TPU:1, one launch (start us, length us, event | category | flops | bytes accessed | tf_op | source)
XLA Modules:
  0.0 72.9 jit_solution(11466276331592912656)
XLA Ops:
  1.3 69.5 %sublayer.1 = (bf16[8,72,128]{2,1,0:T(8,128)(2,1)}, bf16[8,72,128]{2,1,0:T(8,128)(2,1)}, bf16[8,72,128]{2,1,0:T(8,128)(2,1)}, f32[36,36]{1,0:T(8,128)}, f32[1,128]{1,0:T(1,128)}) custom-call(s32[1]{0:T(128)S(6)} %copy.12.len_ref, s32[1,128]{1,0:T(1,128)} %seg_ref.1, bf16[8,72,128]{2,1,0:T(8,128)(2,1)} %bitcast.27, bf16[8,72,128]{2,1,0:T(8,128)(2,1)} %bitcast.28, ...), custom_call_target="tpu_custom_call" | custom-call | tf_op jit(solution)/shard_map/sublayer/pallas_call | solution.py:529
  70.8 2.1 %scale.1 = (f32[576,128]{1,0:T(8,128)}, f32[576,128]{1,0:T(8,128)}, f32[576,128]{1,0:T(8,128)}, f32[36,36]{1,0:T(8,128)}, f32[1,1]{1,0:T(1,128)}) custom-call(f32[1,128]{1,0:T(1,128)} %get-tuple-element.15.sum_ref, bf16[8,72,128]{2,1,0:T(8,128)(2,1)} %get-tuple-element.16.dq_ref, bf16[8,72,128]{2,1,0:T(8,128)(2,1)} %get-tuple-element.17.dk_ref, ...), custom_call_target="tpu_custom_call" | custom-call | tf_op jit(solution)/shard_map/scale/pallas_call | solution.py:621

commit v2 on v1

v2 whole, which is shorter than its diff:
```python
import functools
import math

import jax
import jax.numpy as jnp
from jax import lax
from jax.experimental import pallas as pl
from jax.experimental.pallas import tpu as pltpu
from jax.sharding import PartitionSpec as P

MESH = pl.DeviceIdType.MESH
WIDTH = 1152
HEADS = 8
HEAD_DIM = 72
FEAT = 576
FEAT_PAD = 640
FM = 80
LANES = 128
SPAN = 256
TILE = 256
CHUNK = 512
NEG_LARGE = -1e30
F32 = jnp.float32
BF16 = jnp.bfloat16
XS, ZS = 4, 8
ZH = ZS // 2
X_LANES = 384
Z_LANES = 256
PAIRS = ((4, 0), (3, 5), (2, 6), (1, 7))


def nt(left, right):
    return lax.dot_general(left, right, (((1,), (1,)), ((), ())), preferred_element_type=F32)


def nn(left, right):
    return lax.dot_general(left, right, (((1,), (0,)), ((), ())), preferred_element_type=F32)


def tn(left, right):
    return lax.dot_general(left, right, (((0,), (0,)), ((), ())), preferred_element_type=F32)


def kernel(
    members,
    groups,
    len_ref,
    seg_ref,
    q_ref,
    k_ref,
    v_ref,
    w_hbm,
    t_hbm,
    dq_ref,
    dk_ref,
    dv_ref,
    dw_ref,
    sum_ref,
    q_in,
    k_in,
    v_in,
    w_ref,
    t_ref,
    seg_row,
    seg_all,
    q_slab,
    k_slab,
    v_slab,
    k_tm,
    v_tm,
    k_fm,
    v_fm,
    q_fm,
    g_fm,
    qs_fm,
    gs_fm,
    s_ref,
    p_ref,
    ds_ref,
    att_out,
    attn_all,
    attn_tm,
    attn_in,
    dt_ref,
    dt_in,
    g_out,
    g_slab,
    xv_out,
    xv_in,
    xk_out,
    xk_in,
    v_own,
    k_own,
    oq,
    ok,
    ov,
    xa_ref,
    xa_in,
    za_ref,
    za_in,
    zb_ref,
    zb_in,
    xb_ref,
    xb_in,
    piece_ref,
    yb_ref,
    tile_own,
    tile_all,
    sum_own,
    sum_all,
    load_sem,
    send_sem,
    recv_sem,
    k_recv,
    v_recv,
    q_recv,
    g_recv,
):
    rows = t_ref.shape[0]
    chips = members // 2
    features, share = dw_ref.shape
    me = lax.axis_index("patch")
    dp = lax.axis_index("dp")
    chip, core = me // 2, me % 2
    cx, cz = dp // ZS, dp % ZS
    partner = chip * 2 + 1 - core

    loads = [
        pltpu.make_async_copy(src, dst, load_sem.at[i])
        for i, (src, dst) in enumerate(
            [(seg_ref, seg_row), (k_ref, k_in), (v_ref, v_in), (q_ref, q_in), (w_hbm, w_ref), (t_hbm, t_ref)]
        )
    ]
    for load in loads:
        load.start()

    barrier = pltpu.get_barrier_semaphore()
    for shift in range(1, members):
        pl.semaphore_signal(barrier, inc=1, device_id=(dp, lax.rem(me + shift, members)), device_id_type=MESH)
    for shift in range(1, groups):
        pl.semaphore_signal(barrier, inc=1, device_id=(lax.rem(dp + shift, groups), me), device_id_type=MESH)
    for load in loads[:4]:
        load.wait()
    seg_all[0] = seg_row[...]
    pl.semaphore_wait(barrier, members + groups - 2)

    def copy(src, dst, send, recv, device):
        return pltpu.make_async_remote_copy(
            src_ref=src, dst_ref=dst, send_sem=send, recv_sem=recv, device_id=device, device_id_type=MESH
        )

    def arrived(ref, recv):
        copy(ref, ref, send_sem.at[0], recv, (dp, partner)).wait_recv()

    def sent(ref, send):
        copy(ref, ref, send, recv_sem.at[0], (dp, partner)).wait_send()

    def some(ref, n):
        return ref.at[pl.ds(0, n)]

    SEG, ATTN, XV, XK, DQ, DK, DV, TILE_SUM, ALL_SUM, DT, AT, XA, ZA, ZB, XB, Y, K, V, Q, G = range(20)
    twin = (dp, partner)

    def far(shift):
        return lax.rem(chip + shift, chips)

    def same(shift):
        return (dp, far(shift) * 2 + core)

    def cross(shift):
        return (dp, far(shift) * 2 + 1 - core)

    group_of = {slot: i for i, pair in enumerate(PAIRS) for slot in pair}
    order = [slot for pair in PAIRS for slot in pair if slot]
    position = {slot: i for i, slot in enumerate(slot for pair in PAIRS for slot in pair)}

    for s in order:
        copy(seg_row, seg_all.at[chips - s], send_sem.at[SEG], recv_sem.at[SEG], same(s)).start()
    for s in order + [0]:
        slot = chips + (chips - s) % chips
        copy(seg_row, seg_all.at[slot], send_sem.at[SEG], recv_sem.at[SEG], cross(s)).start()
    for number, source, slab, recv in ((K, k_in, k_slab, k_recv), (V, v_in, v_slab, v_recv)):
        copy(source.at[chip], slab.at[chips], send_sem.at[number], recv.at[len(PAIRS)], twin).start()
    for number, source, slab, recv in ((K, k_in, k_slab, k_recv), (V, v_in, v_slab, v_recv), (Q, q_in, q_slab, q_recv)):
        for s in order:
            slot = chips - s
            copy(source.at[far(s)], slab.at[slot], send_sem.at[number], recv.at[group_of[slot]], same(s)).start()

    length = len_ref[0]
    lane = lax.broadcasted_iota(jnp.int32, (1, rows), 1)
    sublane = lax.broadcasted_iota(jnp.int32, (16, rows), 0)

    def is_group(slot):
        owner = far(slot % chips) * 2 + (core if slot < chips else 1 - core)
        group = jnp.where(owner * rows + lane < length, seg_all[slot], -1) + 1
        return jnp.broadcast_to(group, (16, rows)) == sublane

    zeros40 = jnp.zeros((40, rows), F32)
    zeros48 = jnp.zeros((48, rows), F32)
    zeros8 = jnp.zeros((8, rows), F32)
    ones8 = jnp.ones((8, rows), F32)

    def columns(slot):
        return slice(slot * rows, (slot + 1) * rows)

    def query_columns(slot):
        return columns(position[slot])

    def take_key(slot, value):
        code = jnp.where(is_group(slot), 1.0, 0.0)
        full = jnp.concatenate([value.astype(F32), code, zeros40], axis=0)
        k_fm[:, columns(slot)] = full[:FM].astype(BF16)
        k_tm[columns(slot), :] = full.T.astype(BF16)

    def take_value(slot, value):
        full = jnp.concatenate([value.astype(F32), ones8, zeros48], axis=0)
        v_fm[:, columns(slot)] = full[:FM].astype(BF16)
        v_tm[columns(slot), :] = full.T.astype(BF16)

    def take_query(slot, value):
        code = jnp.where(is_group(slot), 0.0, NEG_LARGE)
        q_fm[:, query_columns(slot)] = jnp.concatenate([value.astype(F32), code, zeros40], axis=0).astype(BF16)

    arrived(some(seg_all, members - 1), recv_sem.at[SEG])

    def gather(number, own, slab, recv, take):
        take(0, own[chip])
        for i, pair in enumerate(PAIRS):
            pair = [slot for slot in pair if slot]
            arrived(some(slab, len(pair)), recv.at[i])
            for slot in pair:
                relay = recv.at[len(PAIRS) + i]
                copy(slab.at[slot], slab.at[chips + slot], send_sem.at[number], relay, twin).start()
            for slot in pair:
                take(slot, slab[slot])

    def gather_twin(slab, recv, take):
        for i, pair in enumerate(PAIRS):
            arrived(some(slab, 2), recv.at[len(PAIRS) + i])
            for slot in pair:
                take(chips + slot, slab[chips + slot])

    gather(K, k_in, k_slab, k_recv, take_key)
    gather_twin(k_slab, k_recv, take_key)
    gather(V, v_in, v_slab, v_recv, take_value)
    gather_twin(v_slab, v_recv, take_value)

    log_scale = math.log2(math.e) / math.sqrt(HEAD_DIM)
    score_scale = 1.0 / math.sqrt(HEAD_DIM)
    total = rows * members
    chunks = [slice(low, low + CHUNK) for low in range(0, total, CHUNK)]

    inverse = {}
    for i, pair in enumerate(PAIRS):
        remote = [slot for slot in pair if slot]
        arrived(some(q_slab, len(remote)), q_recv.at[i])
        for slot in pair:
            take_query(slot, q_slab[slot] if slot else q_in[chip])
        span = slice(i * TILE, (i + 1) * TILE)
        tile = q_fm[:, span]
        top = None
        for chunk in chunks:
            scores = nn(k_tm[chunk, :], tile)
            s_ref[i % 2, chunk, :] = scores
            peak = jnp.max(scores, axis=0, keepdims=True)
            top = peak if top is None else jnp.maximum(top, peak)
        top = top * log_scale
        for chunk in chunks:
            p_ref[chunk, span] = jnp.exp2(s_ref[i % 2, chunk, :] * log_scale - top).astype(BF16)
        accum = nn(v_fm[...], p_ref[:, span])
        for j, slot in enumerate(pair):
            denom = accum[HEAD_DIM : HEAD_DIM + 1, columns(j)]
            inverse[slot] = 1.0 / denom
            attn = (accum[:HEAD_DIM, columns(j)] / denom).astype(BF16)
            att_out[slot] = attn
            if slot:
                copy(att_out.at[slot], attn_all.at[chip], send_sem.at[ATTN], recv_sem.at[ATTN], same(slot)).start()
            else:
                attn_all[chip] = attn
    for slot in range(chips):
        scaled = q_fm[:HEAD_DIM, query_columns(slot)].astype(F32) * (inverse[slot] * score_scale)
        qs_fm[:, query_columns(slot)] = jnp.concatenate([scaled, zeros8], axis=0).astype(BF16)

    loads[4].wait()
    loads[5].wait()
    arrived(some(attn_all, chips - 1), recv_sem.at[ATTN])
    stacked = [attn_all[h].astype(F32) for h in range(HEADS)] + [jnp.zeros((FEAT_PAD - FEAT, rows), F32)]
    attn_tm[...] = jnp.concatenate(stacked, axis=0).T.astype(BF16)
    copy(attn_tm, attn_in, send_sem.at[AT], recv_sem.at[AT], twin).start()
    own_live = me * rows + lax.broadcasted_iota(jnp.int32, (rows, 1), 0) < length
    output = nn(attn_tm[:, :FEAT], w_ref[...])
    error = jnp.where(own_live, output - t_ref[...].astype(F32), 0.0)
    dout_t = (2.0 * error).T
    dout_t = dout_t.astype(BF16)
    dt_ref[...] = dout_t.reshape(dt_ref.shape)
    grad = nn(w_ref[...], dout_t)
    for h in range(HEADS):
        g_out[h] = grad[HEAD_DIM * h : HEAD_DIM * (h + 1)].astype(BF16)
    for s in order:
        slot = chips - s
        copy(g_out.at[far(s)], g_slab.at[slot], send_sem.at[G], g_recv.at[group_of[slot]], same(s)).start()

    for x in range(XS):
        copy(dt_ref.at[2 * x + 1 - core], dt_in.at[x], send_sem.at[DT], recv_sem.at[DT], twin).start()
    loss_part = jnp.sum(jnp.sum(error * error, axis=0, keepdims=True), axis=1, keepdims=True)
    tile_own[...] = jnp.broadcast_to(loss_part, tile_own.shape)
    for shift in range(1, members):
        peer = (dp, lax.rem(me + shift, members))
        copy(tile_own, tile_all.at[members - shift], send_sem.at[TILE_SUM], recv_sem.at[TILE_SUM], peer).start()
    tile_all[0] = tile_own[...]
    arrived(attn_in, recv_sem.at[AT])
    arrived(dt_in, recv_sem.at[DT])
    tall = ZH * share
    left = jnp.concatenate(
        [jnp.concatenate([dt_ref[2 * x + core], dt_in[x]], axis=1) for x in range(XS)], axis=0
    )
    right = jnp.concatenate([attn_tm[...], attn_in[...]], axis=0)
    xa_ref[...] = nn(left, right[:, :X_LANES]).astype(BF16).reshape(XS, tall, X_LANES)
    for d in range(1, XS):
        x = lax.rem(cx + d, XS)
        item = copy(xa_ref.at[x], xa_in.at[XS - d - 1], send_sem.at[XA], recv_sem.at[XA], (x * ZS + cz, me))
        item.start()
    part = nn(left, right[:, X_LANES:])
    for x in range(XS):
        for j in range(ZH):
            low = x * tall + j * share
            za_ref[j, x] = part[low : low + share].astype(BF16)

    def along_z(source, landing, number):
        for j in range(ZH):
            target = ZH * core + j

            @pl.when(target != cz)
            def _():
                slot = lax.rem(cz - target + 2 * ZS - 1, ZS)
                device = (cx * ZS + target, me)
                copy(source.at[j], landing.at[slot], send_sem.at[number], recv_sem.at[number], device).start()

    along_z(za_ref, za_in, ZA)
    near = core == cz // ZH
    away = core != cz // ZH
    mine = lax.rem(cz, ZH)

    def take_grad(slot, value):
        wide = value.astype(F32)
        delta = -jnp.sum(wide * att_out[slot].astype(F32), axis=0, keepdims=True)
        high = delta.astype(BF16).astype(F32)
        middle = (delta - high).astype(BF16).astype(F32)
        low = delta - high - middle
        index = lax.broadcasted_iota(jnp.int32, (8, rows), 0)
        extra = jnp.where(index == 0, high, jnp.where(index == 1, middle, jnp.where(index == 2, low, 0.0)))
        g_fm[:, query_columns(slot)] = jnp.concatenate([wide, extra, zeros48], axis=0).astype(BF16)
        gs_fm[:, query_columns(slot)] = jnp.concatenate([wide * inverse[slot], zeros8], axis=0).astype(BF16)

    def send_home(slot, out, ref, number):
        if slot:
            copy(out.at[slot], ref.at[chip], send_sem.at[number], recv_sem.at[number], same(slot)).start()
        else:
            item = pltpu.make_async_copy(out.at[0], ref.at[chip], load_sem.at[len(local)])
            item.start()
            local.append(item)

    local = []
    for i, pair in enumerate(PAIRS):
        remote = [slot for slot in pair if slot]
        arrived(some(g_slab, len(remote)), g_recv.at[i])
        for slot in pair:
            take_grad(slot, g_slab[slot] if slot else g_out[chip])
        span = slice(i * TILE, (i + 1) * TILE)
        tile = g_fm[:, span]
        for chunk in chunks:
            dprobs = nn(v_tm[chunk, :], tile)
            ds_ref[chunk, span] = (p_ref[chunk, span].astype(F32) * dprobs).astype(BF16)
        dq = nn(k_fm[...], ds_ref[:, span])
        for j, slot in enumerate(pair):
            oq[slot] = (dq[:HEAD_DIM, columns(j)] * (inverse[slot] * score_scale)).astype(BF16)
            send_home(slot, oq, dq_ref, DQ)

    def key_side(left, right_ref, mine, out_ref, in_ref, number):
        for i in list(range(chips, members, 2)) + list(range(0, chips, 2)):
            result = nt(left, right_ref[i * rows : (i + 2) * rows, :])
            target, base = (out_ref, i - chips) if i >= chips else (mine, i)
            for j in range(2):
                target[base + j] = result[:HEAD_DIM, columns(j)]
            if i >= chips:
                pair = pl.ds(base, 2)
                copy(out_ref.at[pair], in_ref.at[pair], send_sem.at[number], recv_sem.at[number], twin).start()

    def key_home(mine, in_ref, number, out, ref, home):
        arrived(in_ref, recv_sem.at[number])
        for slot in order + [0]:
            out[slot] = (mine[slot] + in_ref[slot]).astype(BF16)
            send_home(slot, out, ref, home)

    arrived(some(tile_all, members - 1), recv_sem.at[TILE_SUM])
    pack_loss = tile_all[0]
    for slot in range(1, members):
        pack_loss = pack_loss + tile_all[slot]
    sum_own[...] = jnp.where(lane == 0, pack_loss, length.astype(F32))
    for shift in range(1, groups):
        peer = (lax.rem(dp + shift, groups), me)
        copy(sum_own, sum_all.at[groups - shift], send_sem.at[ALL_SUM], recv_sem.at[ALL_SUM], peer).start()
    sum_all[0] = sum_own[...]

    key_side(gs_fm[...], p_ref, v_own, xv_out, xv_in, XV)
    key_home(v_own, xv_in, XV, ov, dv_ref, DV)

    arrived(xa_in, recv_sem.at[XA])
    summed = xa_ref[cx].astype(F32)
    for i in range(XS - 1):
        summed = summed + xa_in[i].astype(F32)
    for j in range(ZH):
        zb_ref[j] = summed[j * share : (j + 1) * share].astype(BF16)
    along_z(zb_ref, zb_in, ZB)

    key_side(qs_fm[...], ds_ref, k_own, xk_out, xk_in, XK)
    key_home(k_own, xk_in, XK, ok, dk_ref, DK)

    @pl.when(near)
    def _():
        arrived(some(za_in, ZS - 1), recv_sem.at[ZA])
        for x in range(XS):
            summed = za_ref[mine, x].astype(F32)
            for i in range(ZS - 1):
                summed = summed + za_in[i, x].astype(F32)
            xb_ref[x] = summed.astype(BF16)
        for d in range(1, XS):
            x = lax.rem(cx + d, XS)
            item = copy(xb_ref.at[x], xb_in.at[XS - d - 1], send_sem.at[XB], recv_sem.at[XB], (x * ZS + cz, me))
            item.start()

    @pl.when(near)
    def _():
        arrived(some(zb_in, ZS - 1), recv_sem.at[ZB])
        summed = zb_ref[mine].astype(F32)
        for i in range(ZS - 1):
            summed = summed + zb_in[i].astype(F32)
        arrived(xb_in, recv_sem.at[XB])
        other = xb_ref[cx].astype(F32)
        for i in range(XS - 1):
            other = other + xb_in[i].astype(F32)
        whole = jnp.concatenate([summed, other], axis=1)
        turned = jnp.concatenate([whole, jnp.zeros((LANES - share, FEAT_PAD), F32)], axis=0).T
        for t in range(members):
            piece_ref[t] = turned[t * features : (t + 1) * features].astype(BF16)
        for shift in range(1, members):
            target = lax.rem(me + shift, members)
            copy(piece_ref.at[target], yb_ref.at[chip], send_sem.at[Y], recv_sem.at[Y], (dp, target)).start()
        yb_ref[chip] = piece_ref[me]

    arrived(some(sum_all, groups - 1), recv_sem.at[ALL_SUM])
    totals = sum_all[0]
    for slot in range(1, groups):
        totals = totals + sum_all[slot]
    sum_ref[...] = totals

    for ref, number in ((dv_ref, DV), (dq_ref, DQ), (dk_ref, DK)):
        arrived(some(ref, chips - 1), recv_sem.at[number])

    @pl.when(near)
    def _():
        arrived(some(yb_ref, chips - 1), recv_sem.at[Y])

    @pl.when(away)
    def _():
        arrived(yb_ref, recv_sem.at[Y])

    result = yb_ref[0].astype(F32)
    for j in range(1, chips):
        result = result + yb_ref[j].astype(F32)
    dw_ref[...] = result[:, :share]

    for item in local:
        item.wait()
    sent(some(seg_all, members - 1), send_sem.at[SEG])
    sent(some(k_slab, members - 1), send_sem.at[K])
    sent(some(v_slab, members - 1), send_sem.at[V])
    for ref, number in ((q_slab, Q), (attn_all, ATTN), (g_slab, G), (dq_ref, DQ), (dv_ref, DV), (dk_ref, DK)):
        sent(some(ref, chips - 1), send_sem.at[number])
    for ref, number in ((attn_tm, AT), (dt_in, DT), (xv_in, XV), (xk_in, XK)):
        sent(ref, send_sem.at[number])
    sent(some(tile_all, members - 1), send_sem.at[TILE_SUM])
    sent(some(sum_all, groups - 1), send_sem.at[ALL_SUM])

    sent(xa_in, send_sem.at[XA])

    @pl.when(near)
    def _():
        sent(some(za_ref, ZH - 1), send_sem.at[ZA])
        sent(some(zb_ref, ZH - 1), send_sem.at[ZB])
        sent(xb_in, send_sem.at[XB])
        sent(some(piece_ref, members - 1), send_sem.at[Y])

    @pl.when(away)
    def _():
        sent(za_ref, send_sem.at[ZA])
        sent(zb_ref, send_sem.at[ZB])


def scale_kernel(slots, total, sum_ref, dq_ref, dk_ref, dv_ref, dw_ref, query_ref, key_ref, value_ref, weight_ref, loss_ref):
    count = sum_ref[0:1, 1:2]
    ratio = slots / count
    for source, target in ((dq_ref, query_ref), (dk_ref, key_ref), (dv_ref, value_ref)):
        for h in range(HEADS):
            target[HEAD_DIM * h : HEAD_DIM * (h + 1), :] = source[h].astype(F32) * ratio
    weight_ref[...] = dw_ref[...] * (ratio / total)
    loss_ref[...] = sum_ref[0:1, 0:1] / (count * WIDTH)


def solution(mesh):
    members, groups = mesh.shape["patch"], mesh.shape["dp"]

    def local(query_rows, key_rows, value_rows, out_weight, target, lengths, segments):
        rows = query_rows.shape[1]
        total = rows * members
        chips = members // 2
        queries = rows * chips
        share = WIDTH // groups
        vmem = pl.BlockSpec(memory_space=pltpu.VMEM)
        hbm = pl.BlockSpec(memory_space=pltpu.HBM)
        dma = pltpu.SemaphoreType.DMA
        slab = (HEAD_DIM, rows)

        def heads(value):
            return value[0].T.reshape(HEADS, HEAD_DIM, rows)

        def bf(*shape):
            return pltpu.VMEM(shape, BF16)

        def fl(*shape):
            return pltpu.VMEM(shape, F32)

        outs = pl.pallas_call(
            functools.partial(kernel, members, groups),
            out_shape=(
                jax.ShapeDtypeStruct((HEADS, HEAD_DIM, rows), BF16),
                jax.ShapeDtypeStruct((HEADS, HEAD_DIM, rows), BF16),
                jax.ShapeDtypeStruct((HEADS, HEAD_DIM, rows), BF16),
                jax.ShapeDtypeStruct((FEAT // members, share), F32),
                jax.ShapeDtypeStruct((1, LANES), F32),
            ),
            in_specs=[pl.BlockSpec(memory_space=pltpu.SMEM)] + [hbm] * 6,
            out_specs=(hbm, hbm, hbm, vmem, vmem),
            scratch_shapes=[
                bf(HEADS, *slab),
                bf(HEADS, *slab),
                bf(HEADS, *slab),
                bf(FEAT, WIDTH),
                bf(rows, WIDTH),
                pltpu.VMEM((1, rows), jnp.int32),
                pltpu.VMEM((members, 1, rows), jnp.int32),
                bf(chips, *slab),
                bf(members, *slab),
                bf(members, *slab),
                bf(total, LANES),
                bf(total, LANES),
                bf(FM, total),
                bf(FM, total),
                bf(LANES, queries),
                bf(LANES, queries),
                bf(FM, queries),
                bf(FM, queries),
                fl(2, total, TILE),
                bf(total, queries),
                bf(total, queries),
                bf(chips, *slab),
                bf(HEADS, *slab),
                bf(rows, FEAT_PAD),
                bf(rows, FEAT_PAD),
                bf(2 * XS, ZH * share, rows),
                bf(XS, ZH * share, rows),
                bf(HEADS, *slab),
                bf(chips, *slab),
                fl(chips, *slab),
                fl(chips, *slab),
                fl(chips, *slab),
                fl(chips, *slab),
                fl(chips, *slab),
                fl(chips, *slab),
                bf(chips, *slab),
                bf(chips, *slab),
                bf(chips, *slab),
                bf(XS, ZH * share, X_LANES),
                bf(XS - 1, ZH * share, X_LANES),
                bf(ZH, XS, share, Z_LANES),
                bf(ZS, XS, share, Z_LANES),
                bf(ZH, share, X_LANES),
                bf(ZS, share, X_LANES),
                bf(XS, share, Z_LANES),
                bf(XS - 1, share, Z_LANES),
                bf(members, FEAT // members, LANES),
                bf(chips, FEAT // members, LANES),
                fl(1, LANES),
                fl(members, 1, LANES),
                fl(1, LANES),
                fl(groups, 1, LANES),
                dma((6,)),
                dma((20,)),
                dma((16,)),
                dma((2 * len(PAIRS),)),
                dma((2 * len(PAIRS),)),
                dma((len(PAIRS),)),
                dma((len(PAIRS),)),
            ],
            compiler_params=pltpu.CompilerParams(collective_id=0, has_side_effects=True, vmem_limit_bytes=65900000),
            name="sublayer",
        )(
            lengths,
            segments,
            heads(query_rows),
            heads(key_rows),
            heads(value_rows),
            out_weight,
            target[0],
        )
        final = pl.pallas_call(
            functools.partial(scale_kernel, groups * total, total),
            out_shape=(
                jax.ShapeDtypeStruct((FEAT, rows), F32),
                jax.ShapeDtypeStruct((FEAT, rows), F32),
                jax.ShapeDtypeStruct((FEAT, rows), F32),
                jax.ShapeDtypeStruct((FEAT // members, share), F32),
                jax.ShapeDtypeStruct((1, 1), F32),
            ),
            in_specs=[vmem] * 5,
            out_specs=(vmem,) * 5,
            compiler_params=pltpu.CompilerParams(vmem_limit_bytes=65900000),
            name="scale",
        )(outs[4], *outs[:4])
        return (final[0].T[None], final[1].T[None], final[2].T[None], final[3], final[4].reshape(()))

    placed = (
        P("dp", "patch", None),
        P("dp", "patch", None),
        P("dp", "patch", None),
        P(),
        P("dp", "patch", None),
        P("dp"),
        P("dp", "patch"),
    )
    return jax.shard_map(
        local,
        mesh=mesh,
        in_specs=placed,
        out_specs=(
            P("dp", "patch", None),
            P("dp", "patch", None),
            P("dp", "patch", None),
            P("patch", "dp"),
            P(),
        ),
        check_vma=False,
    )
```

time: 73.1 us -> 65.5 us (0.90)
  Pallas kernels: 71.6 us -> 64 us
    pallas_call x1, Pallas kernels: 69.5 us -> 62 us  [local(): pl.pallas_call(functools.partial(kernel, members, groups), out_shape=(jax...]
where the time goes in v2:
time: 65.5 us; the launch traced here: 65.3 us
  Pallas kernels  64 us (98%)
  between operations  1.29 us (2%)
    pallas_call x1, Pallas kernels, local(): pl.pallas_call(functools.partial(kernel, members, groups), out_shape=(jax...  62 us
    pallas_call x1, Pallas kernels, local(): pl.pallas_call(functools.partial(scale_kernel, groups * total, total), ou...  2.07 us

profile of v2, /device:TPU:1, one launch (start us, length us, event | category | flops | bytes accessed | tf_op | source)
XLA Modules:
  0.0 65.3 jit_solution(12634627506789679819)
XLA Ops:
  1.3 62.0 %sublayer.1 = (bf16[8,72,128]{2,1,0:T(8,128)(2,1)}, bf16[8,72,128]{2,1,0:T(8,128)(2,1)}, bf16[8,72,128]{2,1,0:T(8,128)(2,1)}, f32[36,36]{1,0:T(8,128)}, f32[1,128]{1,0:T(1,128)}) custom-call(s32[1]{0:T(128)S(6)} %copy.12.len_ref, s32[1,128]{1,0:T(1,128)} %seg_ref.1, bf16[8,72,128]{2,1,0:T(8,128)(2,1)} %bitcast.27, bf16[8,72,128]{2,1,0:T(8,128)(2,1)} %bitcast.28, ...), custom_call_target="tpu_custom_call" | custom-call | tf_op jit(solution)/shard_map/sublayer/pallas_call | solution.py:533
  63.3 2.1 %scale.1 = (f32[576,128]{1,0:T(8,128)}, f32[576,128]{1,0:T(8,128)}, f32[576,128]{1,0:T(8,128)}, f32[36,36]{1,0:T(8,128)}, f32[1,1]{1,0:T(1,128)}) custom-call(f32[1,128]{1,0:T(1,128)} %get-tuple-element.15.sum_ref, bf16[8,72,128]{2,1,0:T(8,128)(2,1)} %get-tuple-element.16.dq_ref, bf16[8,72,128]{2,1,0:T(8,128)(2,1)} %get-tuple-element.17.dk_ref, ...), custom_call_target="tpu_custom_call" | custom-call | tf_op jit(solution)/shard_map/scale/pallas_call | solution.py:616

commit v3 on v2

--- a/solution.py
+++ b/solution.py
@@ -18,7 +18,7 @@
 LANES = 128
 SPAN = 256
 TILE = 256
-CHUNK = 512
+CHUNK = 256
 NEG_LARGE = -1e30
 F32 = jnp.float32
 BF16 = jnp.bfloat16
@@ -74,7 +74,6 @@
     g_fm,
     qs_fm,
     gs_fm,
-    s_ref,
     p_ref,
     ds_ref,
     att_out,
@@ -193,7 +192,7 @@
     def is_group(slot):
         owner = far(slot % chips) * 2 + (core if slot < chips else 1 - core)
         group = jnp.where(owner * rows + lane < length, seg_all[slot], -1) + 1
-        return jnp.broadcast_to(group, (16, rows)) == sublane
+        return jnp.where(jnp.broadcast_to(group, (16, rows)) == sublane, 1.0, 0.0)
 
     zeros40 = jnp.zeros((40, rows), F32)
     zeros48 = jnp.zeros((48, rows), F32)
@@ -207,8 +206,7 @@
         return columns(position[slot])
 
     def take_key(slot, value):
-        code = jnp.where(is_group(slot), 1.0, 0.0)
-        full = jnp.concatenate([value.astype(F32), code, zeros40], axis=0)
+        full = jnp.concatenate([value.astype(F32), is_group(slot), zeros40], axis=0)
         k_fm[:, columns(slot)] = full[:FM].astype(BF16)
         k_tm[columns(slot), :] = full.T.astype(BF16)
 
@@ -217,9 +215,14 @@
         v_fm[:, columns(slot)] = full[:FM].astype(BF16)
         v_tm[columns(slot), :] = full.T.astype(BF16)
 
-    def take_query(slot, value):
-        code = jnp.where(is_group(slot), 0.0, NEG_LARGE)
-        q_fm[:, query_columns(slot)] = jnp.concatenate([value.astype(F32), code, zeros40], axis=0).astype(BF16)
+    def beside(pair, slots):
+        return jnp.concatenate([slots(slot) for slot in pair], axis=1)
+
+    def take_queries(pair, span):
+        code = (1.0 - beside(pair, is_group)) * NEG_LARGE
+        value = beside(pair, lambda slot: (q_slab[slot] if slot else q_in[chip]).astype(F32))
+        wide40 = jnp.concatenate([zeros40, zeros40], axis=1)
+        q_fm[:, span] = jnp.concatenate([value, code, wide40], axis=0).astype(BF16)
 
     arrived(some(seg_all, members - 1), recv_sem.at[SEG])
 
@@ -250,36 +253,32 @@
     total = rows * members
     chunks = [slice(low, low + CHUNK) for low in range(0, total, CHUNK)]
 
-    inverse = {}
+    inverse = []
     for i, pair in enumerate(PAIRS):
         remote = [slot for slot in pair if slot]
         arrived(some(q_slab, len(remote)), q_recv.at[i])
-        for slot in pair:
-            take_query(slot, q_slab[slot] if slot else q_in[chip])
         span = slice(i * TILE, (i + 1) * TILE)
+        take_queries(pair, span)
         tile = q_fm[:, span]
         top = None
         for chunk in chunks:
-            scores = nn(k_tm[chunk, :], tile)
-            s_ref[i % 2, chunk, :] = scores
-            peak = jnp.max(scores, axis=0, keepdims=True)
+            peak = jnp.max(nn(k_tm[chunk, :], tile), axis=0, keepdims=True)
             top = peak if top is None else jnp.maximum(top, peak)
         top = top * log_scale
         for chunk in chunks:
-            p_ref[chunk, span] = jnp.exp2(s_ref[i % 2, chunk, :] * log_scale - top).astype(BF16)
+            p_ref[chunk, span] = jnp.exp2(nn(k_tm[chunk, :], tile) * log_scale - top).astype(BF16)
         accum = nn(v_fm[...], p_ref[:, span])
+        denom = accum[HEAD_DIM : HEAD_DIM + 1]
+        inverse.append(1.0 / denom)
+        attn = (accum[:HEAD_DIM] / denom).astype(BF16)
         for j, slot in enumerate(pair):
-            denom = accum[HEAD_DIM : HEAD_DIM + 1, columns(j)]
-            inverse[slot] = 1.0 / denom
-            attn = (accum[:HEAD_DIM, columns(j)] / denom).astype(BF16)
-            att_out[slot] = attn
+            att_out[slot] = attn[:, columns(j)]
             if slot:
                 copy(att_out.at[slot], attn_all.at[chip], send_sem.at[ATTN], recv_sem.at[ATTN], same(slot)).start()
             else:
-                attn_all[chip] = attn
-    for slot in range(chips):
-        scaled = q_fm[:HEAD_DIM, query_columns(slot)].astype(F32) * (inverse[slot] * score_scale)
-        qs_fm[:, query_columns(slot)] = jnp.concatenate([scaled, zeros8], axis=0).astype(BF16)
+                attn_all[chip] = attn[:, columns(j)]
+        scaled = q_fm[:HEAD_DIM, span].astype(F32) * (inverse[i] * score_scale)
+        qs_fm[:, span] = jnp.concatenate([scaled, jnp.zeros((FM - HEAD_DIM, TILE), F32)], axis=0).astype(BF16)
 
     loads[4].wait()
     loads[5].wait()
@@ -341,16 +340,18 @@
     away = core != cz // ZH
     mine = lax.rem(cz, ZH)
 
-    def take_grad(slot, value):
-        wide = value.astype(F32)
-        delta = -jnp.sum(wide * att_out[slot].astype(F32), axis=0, keepdims=True)
+    def take_grads(i, pair, span):
+        wide = beside(pair, lambda slot: (g_slab[slot] if slot else g_out[chip]).astype(F32))
+        attn = beside(pair, lambda slot: att_out[slot].astype(F32))
+        delta = -jnp.sum(wide * attn, axis=0, keepdims=True)
         high = delta.astype(BF16).astype(F32)
         middle = (delta - high).astype(BF16).astype(F32)
         low = delta - high - middle
-        index = lax.broadcasted_iota(jnp.int32, (8, rows), 0)
+        index = lax.broadcasted_iota(jnp.int32, (8, TILE), 0)
         extra = jnp.where(index == 0, high, jnp.where(index == 1, middle, jnp.where(index == 2, low, 0.0)))
-        g_fm[:, query_columns(slot)] = jnp.concatenate([wide, extra, zeros48], axis=0).astype(BF16)
-        gs_fm[:, query_columns(slot)] = jnp.concatenate([wide * inverse[slot], zeros8], axis=0).astype(BF16)
+        g_fm[:, span] = jnp.concatenate([wide, extra, jnp.zeros((48, TILE), F32)], axis=0).astype(BF16)
+        scaled = jnp.concatenate([wide * inverse[i], jnp.zeros((FM - HEAD_DIM, TILE), F32)], axis=0)
+        gs_fm[:, span] = scaled.astype(BF16)
 
     def send_home(slot, out, ref, number):
         if slot:
@@ -364,27 +365,27 @@
     for i, pair in enumerate(PAIRS):
         remote = [slot for slot in pair if slot]
         arrived(some(g_slab, len(remote)), g_recv.at[i])
-        for slot in pair:
-            take_grad(slot, g_slab[slot] if slot else g_out[chip])
         span = slice(i * TILE, (i + 1) * TILE)
+        take_grads(i, pair, span)
         tile = g_fm[:, span]
-        for chunk in chunks:
+        for c, chunk in enumerate(chunks):
             dprobs = nn(v_tm[chunk, :], tile)
             ds_ref[chunk, span] = (p_ref[chunk, span].astype(F32) * dprobs).astype(BF16)
         dq = nn(k_fm[...], ds_ref[:, span])
+        dq = (dq[:HEAD_DIM] * (inverse[i] * score_scale)).astype(BF16)
         for j, slot in enumerate(pair):
-            oq[slot] = (dq[:HEAD_DIM, columns(j)] * (inverse[slot] * score_scale)).astype(BF16)
+            oq[slot] = dq[:, columns(j)]
             send_home(slot, oq, dq_ref, DQ)
 
-    def key_side(left, right_ref, mine, out_ref, in_ref, number):
-        for i in list(range(chips, members, 2)) + list(range(0, chips, 2)):
-            result = nt(left, right_ref[i * rows : (i + 2) * rows, :])
-            target, base = (out_ref, i - chips) if i >= chips else (mine, i)
-            for j in range(2):
-                target[base + j] = result[:HEAD_DIM, columns(j)]
-            if i >= chips:
-                pair = pl.ds(base, 2)
-                copy(out_ref.at[pair], in_ref.at[pair], send_sem.at[number], recv_sem.at[number], twin).start()
+    half = len(chunks) // 2
+
+    def key_side(c, left, right_ref, target):
+        result = nt(left, right_ref[chunks[c], :])
+        for j in range(CHUNK // rows):
+            target[(c % half) * (CHUNK // rows) + j] = result[:HEAD_DIM, columns(j)]
+
+    def swap(out_ref, in_ref, number):
+        copy(out_ref, in_ref, send_sem.at[number], recv_sem.at[number], twin).start()
 
     def key_home(mine, in_ref, number, out, ref, home):
         arrived(in_ref, recv_sem.at[number])
@@ -402,9 +403,11 @@
         copy(sum_own, sum_all.at[groups - shift], send_sem.at[ALL_SUM], recv_sem.at[ALL_SUM], peer).start()
     sum_all[0] = sum_own[...]
 
-    key_side(gs_fm[...], p_ref, v_own, xv_out, xv_in, XV)
-    key_home(v_own, xv_in, XV, ov, dv_ref, DV)
-
+    for c in range(half, 2 * half):
+        key_side(c, gs_fm[...], p_ref, xv_out)
+    swap(xv_out, xv_in, XV)
+    for c in range(half):
+        key_side(c, gs_fm[...], p_ref, v_own)
     arrived(xa_in, recv_sem.at[XA])
     summed = xa_ref[cx].astype(F32)
     for i in range(XS - 1):
@@ -413,7 +416,12 @@
         zb_ref[j] = summed[j * share : (j + 1) * share].astype(BF16)
     along_z(zb_ref, zb_in, ZB)
 
-    key_side(qs_fm[...], ds_ref, k_own, xk_out, xk_in, XK)
+    for c in range(half, 2 * half):
+        key_side(c, qs_fm[...], ds_ref, xk_out)
+    swap(xk_out, xk_in, XK)
+    key_home(v_own, xv_in, XV, ov, dv_ref, DV)
+    for c in range(half):
+        key_side(c, qs_fm[...], ds_ref, k_own)
     key_home(k_own, xk_in, XK, ok, dk_ref, DK)
 
     @pl.when(near)
@@ -429,6 +437,8 @@
             item = copy(xb_ref.at[x], xb_in.at[XS - d - 1], send_sem.at[XB], recv_sem.at[XB], (x * ZS + cz, me))
             item.start()
 
+    third = features // 3
+
     @pl.when(near)
     def _():
         arrived(some(zb_in, ZS - 1), recv_sem.at[ZB])
@@ -440,9 +450,10 @@
         for i in range(XS - 1):
             other = other + xb_in[i].astype(F32)
         whole = jnp.concatenate([summed, other], axis=1)
-        turned = jnp.concatenate([whole, jnp.zeros((LANES - share, FEAT_PAD), F32)], axis=0).T
+        rolled = [whole] + [pltpu.roll(whole, FEAT_PAD - third * i, 1) for i in (1, 2)]
+        turned = jnp.concatenate(rolled + [jnp.zeros((LANES - 3 * share, FEAT_PAD), F32)], axis=0).T
         for t in range(members):
-            piece_ref[t] = turned[t * features : (t + 1) * features].astype(BF16)
+            piece_ref[t] = turned[t * features : t * features + third].astype(BF16)
         for shift in range(1, members):
             target = lax.rem(me + shift, members)
             copy(piece_ref.at[target], yb_ref.at[chip], send_sem.at[Y], recv_sem.at[Y], (dp, target)).start()
@@ -468,7 +479,8 @@
     result = yb_ref[0].astype(F32)
     for j in range(1, chips):
         result = result + yb_ref[j].astype(F32)
-    dw_ref[...] = result[:, :share]
+    for i in range(3):
+        dw_ref[i * third : (i + 1) * third, :] = result[:, i * share : (i + 1) * share]
 
     for item in local:
         item.wait()
@@ -560,7 +572,6 @@
                 bf(LANES, queries),
                 bf(FM, queries),
                 bf(FM, queries),
-                fl(2, total, TILE),
                 bf(total, queries),
                 bf(total, queries),
                 bf(chips, *slab),
@@ -588,8 +599,8 @@
                 bf(ZS, share, X_LANES),
                 bf(XS, share, Z_LANES),
                 bf(XS - 1, share, Z_LANES),
-                bf(members, FEAT // members, LANES),
-                bf(chips, FEAT // members, LANES),
+                bf(members, FEAT // members // 3, LANES),
+                bf(chips, FEAT // members // 3, LANES),
                 fl(1, LANES),
                 fl(members, 1, LANES),
                 fl(1, LANES),

time: 65.5 us -> 62.6 us (0.956)
  Pallas kernels: 64 us -> 61.1 us
    pallas_call x1, Pallas kernels: 62 us -> 59 us  [local(): pl.pallas_call(functools.partial(kernel, members, groups), out_shape=(jax...]
where the time goes in v3:
time: 62.6 us; the launch traced here: 62.4 us
  Pallas kernels  61.1 us (98%)
  between operations  1.29 us (2%)
    pallas_call x1, Pallas kernels, local(): pl.pallas_call(functools.partial(kernel, members, groups), out_shape=(jax...  59 us
    pallas_call x1, Pallas kernels, local(): pl.pallas_call(functools.partial(scale_kernel, groups * total, total), ou...  2.07 us

profile of v3, /device:TPU:1, one launch (start us, length us, event | category | flops | bytes accessed | tf_op | source)
XLA Modules:
  0.0 62.4 jit_solution(14854192593211938489)
XLA Ops:
  1.3 59.0 %sublayer.1 = (bf16[8,72,128]{2,1,0:T(8,128)(2,1)}, bf16[8,72,128]{2,1,0:T(8,128)(2,1)}, bf16[8,72,128]{2,1,0:T(8,128)(2,1)}, f32[36,36]{1,0:T(8,128)}, f32[1,128]{1,0:T(1,128)}) custom-call(s32[1]{0:T(128)S(6)} %copy.12.len_ref, s32[1,128]{1,0:T(1,128)} %seg_ref.1, bf16[8,72,128]{2,1,0:T(8,128)(2,1)} %bitcast.27, bf16[8,72,128]{2,1,0:T(8,128)(2,1)} %bitcast.28, ...), custom_call_target="tpu_custom_call" | custom-call | tf_op jit(solution)/shard_map/sublayer/pallas_call | solution.py:545
  60.3 2.1 %scale.1 = (f32[576,128]{1,0:T(8,128)}, f32[576,128]{1,0:T(8,128)}, f32[576,128]{1,0:T(8,128)}, f32[36,36]{1,0:T(8,128)}, f32[1,1]{1,0:T(1,128)}) custom-call(f32[1,128]{1,0:T(1,128)} %get-tuple-element.15.sum_ref, bf16[8,72,128]{2,1,0:T(8,128)(2,1)} %get-tuple-element.16.dq_ref, bf16[8,72,128]{2,1,0:T(8,128)(2,1)} %get-tuple-element.17.dk_ref, ...), custom_call_target="tpu_custom_call" | custom-call | tf_op jit(solution)/shard_map/scale/pallas_call | solution.py:627

commit v4 on v3

--- a/solution.py
+++ b/solution.py
@@ -25,6 +25,7 @@
 XS, ZS = 4, 8
 ZH = ZS // 2
 X_LANES = 384
+LEADER = 1
 Z_LANES = 256
 PAIRS = ((4, 0), (3, 5), (2, 6), (1, 7))
 
@@ -54,8 +55,8 @@
     dq_ref,
     dk_ref,
     dv_ref,
-    dw_ref,
-    sum_ref,
+    yb_ref,
+    sum_all,
     q_in,
     k_in,
     v_in,
@@ -102,11 +103,10 @@
     xb_ref,
     xb_in,
     piece_ref,
-    yb_ref,
     tile_own,
     tile_all,
     sum_own,
-    sum_all,
+    ready,
     load_sem,
     send_sem,
     recv_sem,
@@ -117,7 +117,8 @@
 ):
     rows = t_ref.shape[0]
     chips = members // 2
-    features, share = dw_ref.shape
+    share = WIDTH // groups
+    features = FEAT // members
     me = lax.axis_index("patch")
     dp = lax.axis_index("dp")
     chip, core = me // 2, me % 2
@@ -136,12 +137,24 @@
     barrier = pltpu.get_barrier_semaphore()
     for shift in range(1, members):
         pl.semaphore_signal(barrier, inc=1, device_id=(dp, lax.rem(me + shift, members)), device_id_type=MESH)
-    for shift in range(1, groups):
-        pl.semaphore_signal(barrier, inc=1, device_id=(lax.rem(dp + shift, groups), me), device_id_type=MESH)
     for load in loads[:4]:
         load.wait()
     seg_all[0] = seg_row[...]
-    pl.semaphore_wait(barrier, members + groups - 2)
+    leads = me == LEADER
+
+    @pl.when(jnp.logical_not(leads))
+    def _():
+        pl.semaphore_wait(barrier, members - 1)
+
+    @pl.when(me == LEADER - 1)
+    def _():
+        pl.semaphore_signal(ready, inc=1, device_id=(dp, LEADER), device_id_type=MESH)
+
+    @pl.when(leads)
+    def _():
+        pl.semaphore_wait(ready, 1)
+        for shift in range(1, groups):
+            pl.semaphore_signal(barrier, inc=1, device_id=(lax.rem(dp + shift, groups), me), device_id_type=MESH)
 
     def copy(src, dst, send, recv, device):
         return pltpu.make_async_remote_copy(
@@ -280,6 +293,13 @@
         scaled = q_fm[:HEAD_DIM, span].astype(F32) * (inverse[i] * score_scale)
         qs_fm[:, span] = jnp.concatenate([scaled, jnp.zeros((FM - HEAD_DIM, TILE), F32)], axis=0).astype(BF16)
 
+    @pl.when(leads)
+    def _():
+        pl.semaphore_wait(barrier, members + groups - 2)
+        for shift in range(1, members):
+            peer = (dp, lax.rem(me + shift, members))
+            pl.semaphore_signal(ready, inc=1, device_id=peer, device_id_type=MESH)
+
     loads[4].wait()
     loads[5].wait()
     arrived(some(attn_all, chips - 1), recv_sem.at[ATTN])
@@ -315,6 +335,11 @@
     )
     right = jnp.concatenate([attn_tm[...], attn_in[...]], axis=0)
     xa_ref[...] = nn(left, right[:, :X_LANES]).astype(BF16).reshape(XS, tall, X_LANES)
+
+    @pl.when(jnp.logical_not(leads))
+    def _():
+        pl.semaphore_wait(ready, 1)
+
     for d in range(1, XS):
         x = lax.rem(cx + d, XS)
         item = copy(xa_ref.at[x], xa_in.at[XS - d - 1], send_sem.at[XA], recv_sem.at[XA], (x * ZS + cz, me))
@@ -357,7 +382,7 @@
         if slot:
             copy(out.at[slot], ref.at[chip], send_sem.at[number], recv_sem.at[number], same(slot)).start()
         else:
-            item = pltpu.make_async_copy(out.at[0], ref.at[chip], load_sem.at[len(local)])
+            item = pltpu.make_async_copy(out.at[0], ref.at[chip], load_sem.at[(DQ, DV, DK).index(number)])
             item.start()
             local.append(item)
 
@@ -401,7 +426,8 @@
     for shift in range(1, groups):
         peer = (lax.rem(dp + shift, groups), me)
         copy(sum_own, sum_all.at[groups - shift], send_sem.at[ALL_SUM], recv_sem.at[ALL_SUM], peer).start()
-    sum_all[0] = sum_own[...]
+    local.append(pltpu.make_async_copy(sum_own, sum_all.at[0], load_sem.at[3]))
+    local[-1].start()
 
     for c in range(half, 2 * half):
         key_side(c, gs_fm[...], p_ref, xv_out)
@@ -457,13 +483,9 @@
         for shift in range(1, members):
             target = lax.rem(me + shift, members)
             copy(piece_ref.at[target], yb_ref.at[chip], send_sem.at[Y], recv_sem.at[Y], (dp, target)).start()
-        yb_ref[chip] = piece_ref[me]
+        pltpu.make_async_copy(piece_ref.at[me], yb_ref.at[chip], load_sem.at[4]).start()
 
     arrived(some(sum_all, groups - 1), recv_sem.at[ALL_SUM])
-    totals = sum_all[0]
-    for slot in range(1, groups):
-        totals = totals + sum_all[slot]
-    sum_ref[...] = totals
 
     for ref, number in ((dv_ref, DV), (dq_ref, DQ), (dk_ref, DK)):
         arrived(some(ref, chips - 1), recv_sem.at[number])
@@ -471,16 +493,11 @@
     @pl.when(near)
     def _():
         arrived(some(yb_ref, chips - 1), recv_sem.at[Y])
+        pltpu.make_async_copy(piece_ref.at[me], yb_ref.at[chip], load_sem.at[4]).wait()
 
     @pl.when(away)
     def _():
         arrived(yb_ref, recv_sem.at[Y])
-
-    result = yb_ref[0].astype(F32)
-    for j in range(1, chips):
-        result = result + yb_ref[j].astype(F32)
-    for i in range(3):
-        dw_ref[i * third : (i + 1) * third, :] = result[:, i * share : (i + 1) * share]
 
     for item in local:
         item.wait()
@@ -509,14 +526,55 @@
         sent(zb_ref, send_sem.at[ZB])
 
 
-def scale_kernel(slots, total, sum_ref, dq_ref, dk_ref, dv_ref, dw_ref, query_ref, key_ref, value_ref, weight_ref, loss_ref):
-    count = sum_ref[0:1, 1:2]
+def scale_kernel(
+    slots,
+    total,
+    sum_hbm,
+    dq_hbm,
+    dk_hbm,
+    dv_hbm,
+    yb_hbm,
+    query_hbm,
+    key_hbm,
+    value_hbm,
+    weight_ref,
+    loss_ref,
+    sum_ref,
+    slab_ref,
+    yb_ref,
+    out_ref,
+    in_sem,
+    out_sem,
+):
+    sources = [(sum_hbm, sum_ref), (yb_hbm, yb_ref)]
+    sources += [(ref, slab_ref.at[i]) for i, ref in enumerate((dv_hbm, dq_hbm, dk_hbm))]
+    loads = [pltpu.make_async_copy(src, dst, in_sem.at[i]) for i, (src, dst) in enumerate(sources)]
+    for load in loads:
+        load.start()
+    loads[0].wait()
+    totals = sum_ref[0]
+    for i in range(1, sum_ref.shape[0]):
+        totals = totals + sum_ref[i]
+    count = totals[:, 1:2]
     ratio = slots / count
-    for source, target in ((dq_ref, query_ref), (dk_ref, key_ref), (dv_ref, value_ref)):
+    stores = []
+    for i, target in enumerate((value_hbm, query_hbm, key_hbm)):
+        loads[i + 2].wait()
         for h in range(HEADS):
-            target[HEAD_DIM * h : HEAD_DIM * (h + 1), :] = source[h].astype(F32) * ratio
-    weight_ref[...] = dw_ref[...] * (ratio / total)
-    loss_ref[...] = sum_ref[0:1, 0:1] / (count * WIDTH)
+            out_ref[i, HEAD_DIM * h : HEAD_DIM * (h + 1), :] = slab_ref[i, h].astype(F32) * ratio
+        stores.append(pltpu.make_async_copy(out_ref.at[i], target, out_sem.at[i]))
+        stores[-1].start()
+    loads[1].wait()
+    result = yb_ref[0].astype(F32)
+    for i in range(1, yb_ref.shape[0]):
+        result = result + yb_ref[i].astype(F32)
+    result = result * (ratio / total)
+    third, share = result.shape[0], weight_ref.shape[1]
+    for i in range(3):
+        weight_ref[i * third : (i + 1) * third, :] = result[:, i * share : (i + 1) * share]
+    loss_ref[...] = totals[:, 0:1] / (count * WIDTH)
+    for store in stores:
+        store.wait()
 
 
 def solution(mesh):
@@ -548,11 +606,11 @@
                 jax.ShapeDtypeStruct((HEADS, HEAD_DIM, rows), BF16),
                 jax.ShapeDtypeStruct((HEADS, HEAD_DIM, rows), BF16),
                 jax.ShapeDtypeStruct((HEADS, HEAD_DIM, rows), BF16),
-                jax.ShapeDtypeStruct((FEAT // members, share), F32),
-                jax.ShapeDtypeStruct((1, LANES), F32),
+                jax.ShapeDtypeStruct((chips, FEAT // members // 3, LANES), BF16),
+                jax.ShapeDtypeStruct((groups, 1, LANES), F32),
             ),
             in_specs=[pl.BlockSpec(memory_space=pltpu.SMEM)] + [hbm] * 6,
-            out_specs=(hbm, hbm, hbm, vmem, vmem),
+            out_specs=(hbm,) * 5,
             scratch_shapes=[
                 bf(HEADS, *slab),
                 bf(HEADS, *slab),
@@ -600,11 +658,10 @@
                 bf(XS, share, Z_LANES),
                 bf(XS - 1, share, Z_LANES),
                 bf(members, FEAT // members // 3, LANES),
-                bf(chips, FEAT // members // 3, LANES),
                 fl(1, LANES),
                 fl(members, 1, LANES),
                 fl(1, LANES),
-                fl(groups, 1, LANES),
+                pltpu.SemaphoreType.REGULAR,
                 dma((6,)),
                 dma((20,)),
                 dma((16,)),
@@ -633,8 +690,16 @@
                 jax.ShapeDtypeStruct((FEAT // members, share), F32),
                 jax.ShapeDtypeStruct((1, 1), F32),
             ),
-            in_specs=[vmem] * 5,
-            out_specs=(vmem,) * 5,
+            in_specs=[hbm] * 5,
+            out_specs=(hbm, hbm, hbm, vmem, vmem),
+            scratch_shapes=[
+                fl(groups, 1, LANES),
+                bf(3, HEADS, *slab),
+                bf(chips, FEAT // members // 3, LANES),
+                fl(3, FEAT, rows),
+                dma((5,)),
+                dma((3,)),
+            ],
             compiler_params=pltpu.CompilerParams(vmem_limit_bytes=65900000),
             name="scale",
         )(outs[4], *outs[:4])

time: 62.6 us -> 60.5 us (0.966)
  Pallas kernels: 61.1 us -> 58.9 us
    pallas_call x1, Pallas kernels: 59 us -> 56.3 us  [local(): pl.pallas_call(functools.partial(kernel, members, groups), out_shape=(jax...]
where the time goes in v4:
time: 60.5 us; the launch traced here: 60.2 us
  Pallas kernels  58.9 us (97%)
  between operations  1.29 us (2%)
    pallas_call x1, Pallas kernels, local(): pl.pallas_call(functools.partial(kernel, members, groups), out_shape=(jax...  56.3 us
    pallas_call x1, Pallas kernels, local(): pl.pallas_call(functools.partial(scale_kernel, groups * total, total), ou...  2.62 us

profile of v4, /device:TPU:1, one launch (start us, length us, event | category | flops | bytes accessed | tf_op | source)
XLA Modules:
  0.0 60.2 jit_solution(11540989886130775094)
XLA Ops:
  1.3 56.3 %sublayer.1 = (bf16[8,72,128]{2,1,0:T(8,128)(2,1)}, bf16[8,72,128]{2,1,0:T(8,128)(2,1)}, bf16[8,72,128]{2,1,0:T(8,128)(2,1)}, bf16[8,12,128]{2,1,0:T(8,128)(2,1)}, f32[32,1,128]{2,1,0:T(1,128)}) custom-call(s32[1]{0:T(128)S(6)} %copy.12.len_ref, s32[1,128]{1,0:T(1,128)} %seg_ref.1, bf16[8,72,128]{2,1,0:T(8,128)(2,1)} %bitcast.27, ...), custom_call_target="tpu_custom_call" | custom-call | tf_op jit(solution)/shard_map/sublayer/pallas_call | solution.py:603
  57.6 2.6 %scale.1 = (f32[576,128]{1,0:T(8,128)}, f32[576,128]{1,0:T(8,128)}, f32[576,128]{1,0:T(8,128)}, f32[36,36]{1,0:T(8,128)}, f32[1,1]{1,0:T(1,128)}) custom-call(f32[32,1,128]{2,1,0:T(1,128)} %get-tuple-element.15.sum_hbm, bf16[8,72,128]{2,1,0:T(8,128)(2,1)} %get-tuple-element.16.dq_hbm, bf16[8,72,128]{2,1,0:T(8,128)(2,1)} %get-tuple-element.17.dk_hbm, ...), custom_call_target="tpu_custom_call" | custom-call | tf_op jit(solution)/shard_map/scale/pallas_call | solution.py:684

commit v5 on v4

--- a/solution.py
+++ b/solution.py
@@ -90,6 +90,7 @@
     xk_out,
     xk_in,
     v_own,
+    v_twin,
     k_own,
     oq,
     ok,
@@ -176,34 +177,37 @@
     def far(shift):
         return lax.rem(chip + shift, chips)
 
-    def same(shift):
-        return (dp, far(shift) * 2 + core)
-
-    def cross(shift):
-        return (dp, far(shift) * 2 + 1 - core)
+    def index_of(shift, flip):
+        return far(shift) * 2 + (1 - core if flip else core)
+
+    def peer_of(shift):
+        return (dp, index_of(shift, True))
+
+    def other_of(shift):
+        return (dp, index_of(shift, not shift))
 
     group_of = {slot: i for i, pair in enumerate(PAIRS) for slot in pair}
     order = [slot for pair in PAIRS for slot in pair if slot]
     position = {slot: i for i, slot in enumerate(slot for pair in PAIRS for slot in pair)}
 
     for s in order:
-        copy(seg_row, seg_all.at[chips - s], send_sem.at[SEG], recv_sem.at[SEG], same(s)).start()
+        copy(seg_row, seg_all.at[chips - s], send_sem.at[SEG], recv_sem.at[SEG], peer_of(s)).start()
     for s in order + [0]:
         slot = chips + (chips - s) % chips
-        copy(seg_row, seg_all.at[slot], send_sem.at[SEG], recv_sem.at[SEG], cross(s)).start()
+        copy(seg_row, seg_all.at[slot], send_sem.at[SEG], recv_sem.at[SEG], other_of(s)).start()
     for number, source, slab, recv in ((K, k_in, k_slab, k_recv), (V, v_in, v_slab, v_recv)):
         copy(source.at[chip], slab.at[chips], send_sem.at[number], recv.at[len(PAIRS)], twin).start()
     for number, source, slab, recv in ((K, k_in, k_slab, k_recv), (V, v_in, v_slab, v_recv), (Q, q_in, q_slab, q_recv)):
         for s in order:
             slot = chips - s
-            copy(source.at[far(s)], slab.at[slot], send_sem.at[number], recv.at[group_of[slot]], same(s)).start()
+            copy(source.at[far(s)], slab.at[slot], send_sem.at[number], recv.at[group_of[slot]], peer_of(s)).start()
 
     length = len_ref[0]
     lane = lax.broadcasted_iota(jnp.int32, (1, rows), 1)
     sublane = lax.broadcasted_iota(jnp.int32, (16, rows), 0)
 
     def is_group(slot):
-        owner = far(slot % chips) * 2 + (core if slot < chips else 1 - core)
+        owner = index_of(slot % chips, (slot % chips > 0) == (slot < chips))
         group = jnp.where(owner * rows + lane < length, seg_all[slot], -1) + 1
         return jnp.where(jnp.broadcast_to(group, (16, rows)) == sublane, 1.0, 0.0)
 
@@ -287,7 +291,7 @@
         for j, slot in enumerate(pair):
             att_out[slot] = attn[:, columns(j)]
             if slot:
-                copy(att_out.at[slot], attn_all.at[chip], send_sem.at[ATTN], recv_sem.at[ATTN], same(slot)).start()
+                copy(att_out.at[slot], attn_all.at[chip], send_sem.at[ATTN], recv_sem.at[ATTN], peer_of(slot)).start()
             else:
                 attn_all[chip] = attn[:, columns(j)]
         scaled = q_fm[:HEAD_DIM, span].astype(F32) * (inverse[i] * score_scale)
@@ -312,15 +316,15 @@
     dout_t = (2.0 * error).T
     dout_t = dout_t.astype(BF16)
     dt_ref[...] = dout_t.reshape(dt_ref.shape)
+    for x in range(XS):
+        copy(dt_ref.at[2 * x + 1 - core], dt_in.at[x], send_sem.at[DT], recv_sem.at[DT], twin).start()
     grad = nn(w_ref[...], dout_t)
     for h in range(HEADS):
         g_out[h] = grad[HEAD_DIM * h : HEAD_DIM * (h + 1)].astype(BF16)
-    for s in order:
+    for s in order[::-1]:
         slot = chips - s
-        copy(g_out.at[far(s)], g_slab.at[slot], send_sem.at[G], g_recv.at[group_of[slot]], same(s)).start()
-
-    for x in range(XS):
-        copy(dt_ref.at[2 * x + 1 - core], dt_in.at[x], send_sem.at[DT], recv_sem.at[DT], twin).start()
+        copy(g_out.at[far(s)], g_slab.at[slot], send_sem.at[G], g_recv.at[group_of[slot]], peer_of(s)).start()
+
     loss_part = jnp.sum(jnp.sum(error * error, axis=0, keepdims=True), axis=1, keepdims=True)
     tile_own[...] = jnp.broadcast_to(loss_part, tile_own.shape)
     for shift in range(1, members):
@@ -380,20 +384,54 @@
 
     def send_home(slot, out, ref, number):
         if slot:
-            copy(out.at[slot], ref.at[chip], send_sem.at[number], recv_sem.at[number], same(slot)).start()
+            copy(out.at[slot], ref.at[chip], send_sem.at[number], recv_sem.at[number], peer_of(slot)).start()
         else:
             item = pltpu.make_async_copy(out.at[0], ref.at[chip], load_sem.at[(DQ, DV, DK).index(number)])
             item.start()
             local.append(item)
 
     local = []
-    for i, pair in enumerate(PAIRS):
+    half = len(chunks) // 2
+    each = CHUNK // rows
+
+    def key_side(c, left, right, target, base=None):
+        result = nt(left, right)[:HEAD_DIM]
+        for j in range(each):
+            slot = (c % half) * each + j
+            value = result[:, columns(j)]
+            target[slot] = value if base is None else base[slot] + value
+
+    def swap(out_ref, in_ref, number):
+        copy(out_ref, in_ref, send_sem.at[number], recv_sem.at[number], twin).start()
+
+    def key_home(mine, in_ref, number, out, ref, home):
+        arrived(in_ref, recv_sem.at[number])
+        for slot in order + [0]:
+            out[slot] = (mine[slot] + in_ref[slot]).astype(BF16)
+            send_home(slot, out, ref, home)
+
+    for i, pair in list(enumerate(PAIRS))[::-1]:
         remote = [slot for slot in pair if slot]
         arrived(some(g_slab, len(remote)), g_recv.at[i])
         span = slice(i * TILE, (i + 1) * TILE)
         take_grads(i, pair, span)
+        first, last = i == len(PAIRS) - 1, i == 0
+        for c in list(range(half, 2 * half)) + list(range(half)):
+            side = v_twin if c >= half else v_own
+            target = xv_out if c >= half and last else side
+            key_side(c, gs_fm[:, span], p_ref[chunks[c], span], target, None if first else side)
+            if last and c == 2 * half - 1:
+                swap(xv_out, xv_in, XV)
+        if last:
+            arrived(xa_in, recv_sem.at[XA])
+            summed = xa_ref[cx].astype(F32)
+            for d in range(XS - 1):
+                summed = summed + xa_in[d].astype(F32)
+            for j in range(ZH):
+                zb_ref[j] = summed[j * share : (j + 1) * share].astype(BF16)
+            along_z(zb_ref, zb_in, ZB)
         tile = g_fm[:, span]
-        for c, chunk in enumerate(chunks):
+        for chunk in chunks:
             dprobs = nn(v_tm[chunk, :], tile)
             ds_ref[chunk, span] = (p_ref[chunk, span].astype(F32) * dprobs).astype(BF16)
         dq = nn(k_fm[...], ds_ref[:, span])
@@ -402,22 +440,10 @@
             oq[slot] = dq[:, columns(j)]
             send_home(slot, oq, dq_ref, DQ)
 
-    half = len(chunks) // 2
-
-    def key_side(c, left, right_ref, target):
-        result = nt(left, right_ref[chunks[c], :])
-        for j in range(CHUNK // rows):
-            target[(c % half) * (CHUNK // rows) + j] = result[:HEAD_DIM, columns(j)]
-
-    def swap(out_ref, in_ref, number):
-        copy(out_ref, in_ref, send_sem.at[number], recv_sem.at[number], twin).start()
-
-    def key_home(mine, in_ref, number, out, ref, home):
-        arrived(in_ref, recv_sem.at[number])
-        for slot in order + [0]:
-            out[slot] = (mine[slot] + in_ref[slot]).astype(BF16)
-            send_home(slot, out, ref, home)
-
+    key_home(v_own, xv_in, XV, ov, dv_ref, DV)
+    for c in range(half, 2 * half):
+        key_side(c, qs_fm[...], ds_ref[chunks[c], :], xk_out)
+    swap(xk_out, xk_in, XK)
     arrived(some(tile_all, members - 1), recv_sem.at[TILE_SUM])
     pack_loss = tile_all[0]
     for slot in range(1, members):
@@ -429,25 +455,8 @@
     local.append(pltpu.make_async_copy(sum_own, sum_all.at[0], load_sem.at[3]))
     local[-1].start()
 
-    for c in range(half, 2 * half):
-        key_side(c, gs_fm[...], p_ref, xv_out)
-    swap(xv_out, xv_in, XV)
     for c in range(half):
-        key_side(c, gs_fm[...], p_ref, v_own)
-    arrived(xa_in, recv_sem.at[XA])
-    summed = xa_ref[cx].astype(F32)
-    for i in range(XS - 1):
-        summed = summed + xa_in[i].astype(F32)
-    for j in range(ZH):
-        zb_ref[j] = summed[j * share : (j + 1) * share].astype(BF16)
-    along_z(zb_ref, zb_in, ZB)
-
-    for c in range(half, 2 * half):
-        key_side(c, qs_fm[...], ds_ref, xk_out)
-    swap(xk_out, xk_in, XK)
-    key_home(v_own, xv_in, XV, ov, dv_ref, DV)
-    for c in range(half):
-        key_side(c, qs_fm[...], ds_ref, k_own)
+        key_side(c, qs_fm[...], ds_ref[chunks[c], :], k_own)
     key_home(k_own, xk_in, XK, ok, dk_ref, DK)
 
     @pl.when(near)
@@ -640,6 +649,7 @@
                 bf(XS, ZH * share, rows),
                 bf(HEADS, *slab),
                 bf(chips, *slab),
+                fl(chips, *slab),
                 fl(chips, *slab),
                 fl(chips, *slab),
                 fl(chips, *slab),

time: 60.5 us -> 60.2 us (level)
  Pallas kernels: 58.9 us -> 58.1 us
    pallas_call x1, Pallas kernels: 56.3 us -> 55.5 us  [local(): pl.pallas_call(functools.partial(kernel, members, groups), out_shape=(jax...]
where the time goes in v5:
time: 60.2 us; the launch traced here: 59.4 us
  Pallas kernels  58.1 us (97%)
  between operations  1.29 us (2%)
    pallas_call x1, Pallas kernels, local(): pl.pallas_call(functools.partial(kernel, members, groups), out_shape=(jax...  55.5 us
    pallas_call x1, Pallas kernels, local(): pl.pallas_call(functools.partial(scale_kernel, groups * total, total), ou...  2.62 us

profile of v5, /device:TPU:1, one launch (start us, length us, event | category | flops | bytes accessed | tf_op | source)
XLA Modules:
  0.0 59.4 jit_solution(4912418817142996329)
XLA Ops:
  1.3 55.5 %sublayer.1 = (bf16[8,72,128]{2,1,0:T(8,128)(2,1)}, bf16[8,72,128]{2,1,0:T(8,128)(2,1)}, bf16[8,72,128]{2,1,0:T(8,128)(2,1)}, bf16[8,12,128]{2,1,0:T(8,128)(2,1)}, f32[32,1,128]{2,1,0:T(1,128)}) custom-call(s32[1]{0:T(128)S(6)} %copy.12.len_ref, s32[1,128]{1,0:T(1,128)} %seg_ref.1, bf16[8,72,128]{2,1,0:T(8,128)(2,1)} %bitcast.27, ...), custom_call_target="tpu_custom_call" | custom-call | tf_op jit(solution)/shard_map/sublayer/pallas_call | solution.py:612
  56.8 2.6 %scale.1 = (f32[576,128]{1,0:T(8,128)}, f32[576,128]{1,0:T(8,128)}, f32[576,128]{1,0:T(8,128)}, f32[36,36]{1,0:T(8,128)}, f32[1,1]{1,0:T(1,128)}) custom-call(f32[32,1,128]{2,1,0:T(1,128)} %get-tuple-element.15.sum_hbm, bf16[8,72,128]{2,1,0:T(8,128)(2,1)} %get-tuple-element.16.dq_hbm, bf16[8,72,128]{2,1,0:T(8,128)(2,1)} %get-tuple-element.17.dk_hbm, ...), custom_call_target="tpu_custom_call" | custom-call | tf_op jit(solution)/shard_map/scale/pallas_call | solution.py:694

commit v6 on v5

--- a/solution.py
+++ b/solution.py
@@ -125,6 +125,7 @@
     chip, core = me // 2, me % 2
     cx, cz = dp // ZS, dp % ZS
     partner = chip * 2 + 1 - core
+    side = 1 - core
 
     loads = [
         pltpu.make_async_copy(src, dst, load_sem.at[i])
@@ -317,7 +318,7 @@
     dout_t = dout_t.astype(BF16)
     dt_ref[...] = dout_t.reshape(dt_ref.shape)
     for x in range(XS):
-        copy(dt_ref.at[2 * x + 1 - core], dt_in.at[x], send_sem.at[DT], recv_sem.at[DT], twin).start()
+        copy(dt_ref.at[2 * x + 1 - side], dt_in.at[x], send_sem.at[DT], recv_sem.at[DT], twin).start()
     grad = nn(w_ref[...], dout_t)
     for h in range(HEADS):
         g_out[h] = grad[HEAD_DIM * h : HEAD_DIM * (h + 1)].astype(BF16)
@@ -335,7 +336,7 @@
     arrived(dt_in, recv_sem.at[DT])
     tall = ZH * share
     left = jnp.concatenate(
-        [jnp.concatenate([dt_ref[2 * x + core], dt_in[x]], axis=1) for x in range(XS)], axis=0
+        [jnp.concatenate([dt_ref[2 * x + side], dt_in[x]], axis=1) for x in range(XS)], axis=0
     )
     right = jnp.concatenate([attn_tm[...], attn_in[...]], axis=0)
     xa_ref[...] = nn(left, right[:, :X_LANES]).astype(BF16).reshape(XS, tall, X_LANES)
@@ -356,7 +357,7 @@
 
     def along_z(source, landing, number):
         for j in range(ZH):
-            target = ZH * core + j
+            target = ZH * side + j
 
             @pl.when(target != cz)
             def _():
@@ -365,8 +366,8 @@
                 copy(source.at[j], landing.at[slot], send_sem.at[number], recv_sem.at[number], device).start()
 
     along_z(za_ref, za_in, ZA)
-    near = core == cz // ZH
-    away = core != cz // ZH
+    near = side == cz // ZH
+    away = side != cz // ZH
     mine = lax.rem(cz, ZH)
 
     def take_grads(i, pair, span):
@@ -417,12 +418,22 @@
         take_grads(i, pair, span)
         first, last = i == len(PAIRS) - 1, i == 0
         for c in list(range(half, 2 * half)) + list(range(half)):
-            side = v_twin if c >= half else v_own
-            target = xv_out if c >= half and last else side
-            key_side(c, gs_fm[:, span], p_ref[chunks[c], span], target, None if first else side)
+            base = v_twin if c >= half else v_own
+            target = xv_out if c >= half and last else base
+            key_side(c, gs_fm[:, span], p_ref[chunks[c], span], target, None if first else base)
             if last and c == 2 * half - 1:
                 swap(xv_out, xv_in, XV)
         if last:
+            arrived(some(tile_all, members - 1), recv_sem.at[TILE_SUM])
+            pack_loss = tile_all[0]
+            for slot in range(1, members):
+                pack_loss = pack_loss + tile_all[slot]
+            sum_own[...] = jnp.where(lane == 0, pack_loss, length.astype(F32))
+            for shift in range(1, groups):
+                peer = (lax.rem(dp + shift, groups), me)
+                copy(sum_own, sum_all.at[groups - shift], send_sem.at[ALL_SUM], recv_sem.at[ALL_SUM], peer).start()
+            local.append(pltpu.make_async_copy(sum_own, sum_all.at[0], load_sem.at[3]))
+            local[-1].start()
             arrived(xa_in, recv_sem.at[XA])
             summed = xa_ref[cx].astype(F32)
             for d in range(XS - 1):
@@ -444,17 +455,6 @@
     for c in range(half, 2 * half):
         key_side(c, qs_fm[...], ds_ref[chunks[c], :], xk_out)
     swap(xk_out, xk_in, XK)
-    arrived(some(tile_all, members - 1), recv_sem.at[TILE_SUM])
-    pack_loss = tile_all[0]
-    for slot in range(1, members):
-        pack_loss = pack_loss + tile_all[slot]
-    sum_own[...] = jnp.where(lane == 0, pack_loss, length.astype(F32))
-    for shift in range(1, groups):
-        peer = (lax.rem(dp + shift, groups), me)
-        copy(sum_own, sum_all.at[groups - shift], send_sem.at[ALL_SUM], recv_sem.at[ALL_SUM], peer).start()
-    local.append(pltpu.make_async_copy(sum_own, sum_all.at[0], load_sem.at[3]))
-    local[-1].start()
-
     for c in range(half):
         key_side(c, qs_fm[...], ds_ref[chunks[c], :], k_own)
     key_home(k_own, xk_in, XK, ok, dk_ref, DK)
@@ -546,34 +546,43 @@
     query_hbm,
     key_hbm,
     value_hbm,
-    weight_ref,
-    loss_ref,
+    weight_hbm,
+    loss_hbm,
     sum_ref,
     slab_ref,
     yb_ref,
     out_ref,
+    weight_ref,
+    loss_ref,
     in_sem,
     out_sem,
 ):
-    sources = [(sum_hbm, sum_ref), (yb_hbm, yb_ref)]
-    sources += [(ref, slab_ref.at[i]) for i, ref in enumerate((dv_hbm, dq_hbm, dk_hbm))]
-    loads = [pltpu.make_async_copy(src, dst, in_sem.at[i]) for i, (src, dst) in enumerate(sources)]
-    for load in loads:
-        load.start()
-    loads[0].wait()
+    def fetch(src, dst, i):
+        return pltpu.make_async_copy(src, dst, in_sem.at[i])
+
+    fetch(sum_hbm, sum_ref, 0).start()
+    grads = list(enumerate(((dv_hbm, value_hbm), (dq_hbm, query_hbm), (dk_hbm, key_hbm))))
+    pieces = [pl.ds(h, 2) for h in range(0, HEADS, 2)]
+    for i, (source, _) in grads:
+        for piece in pieces:
+            fetch(source.at[piece], slab_ref.at[i, piece], i + 2).start()
+    fetch(yb_hbm, yb_ref, 1).start()
+    fetch(sum_hbm, sum_ref, 0).wait()
     totals = sum_ref[0]
     for i in range(1, sum_ref.shape[0]):
         totals = totals + sum_ref[i]
     count = totals[:, 1:2]
     ratio = slots / count
     stores = []
-    for i, target in enumerate((value_hbm, query_hbm, key_hbm)):
-        loads[i + 2].wait()
+    for i, (source, target) in grads:
+        fetch(source, slab_ref.at[i], i + 2).wait()
         for h in range(HEADS):
             out_ref[i, HEAD_DIM * h : HEAD_DIM * (h + 1), :] = slab_ref[i, h].astype(F32) * ratio
+            if h % 2:
+                part = pl.ds(HEAD_DIM * (h - 1), 2 * HEAD_DIM)
+                pltpu.make_async_copy(out_ref.at[i, part], target.at[part], out_sem.at[i]).start()
         stores.append(pltpu.make_async_copy(out_ref.at[i], target, out_sem.at[i]))
-        stores[-1].start()
-    loads[1].wait()
+    fetch(yb_hbm, yb_ref, 1).wait()
     result = yb_ref[0].astype(F32)
     for i in range(1, yb_ref.shape[0]):
         result = result + yb_ref[i].astype(F32)
@@ -582,6 +591,9 @@
     for i in range(3):
         weight_ref[i * third : (i + 1) * third, :] = result[:, i * share : (i + 1) * share]
     loss_ref[...] = totals[:, 0:1] / (count * WIDTH)
+    for i, (source, target) in enumerate(((weight_ref, weight_hbm), (loss_ref, loss_hbm))):
+        stores.append(pltpu.make_async_copy(source, target, out_sem.at[3 + i]))
+        stores[-1].start()
     for store in stores:
         store.wait()
 
@@ -595,7 +607,6 @@
         chips = members // 2
         queries = rows * chips
         share = WIDTH // groups
-        vmem = pl.BlockSpec(memory_space=pltpu.VMEM)
         hbm = pl.BlockSpec(memory_space=pltpu.HBM)
         dma = pltpu.SemaphoreType.DMA
         slab = (HEAD_DIM, rows)
@@ -701,14 +712,16 @@
                 jax.ShapeDtypeStruct((1, 1), F32),
             ),
             in_specs=[hbm] * 5,
-            out_specs=(hbm, hbm, hbm, vmem, vmem),
+            out_specs=(hbm,) * 5,
             scratch_shapes=[
                 fl(groups, 1, LANES),
                 bf(3, HEADS, *slab),
                 bf(chips, FEAT // members // 3, LANES),
                 fl(3, FEAT, rows),
+                fl(FEAT // members, share),
+                fl(1, 1),
                 dma((5,)),
-                dma((3,)),
+                dma((5,)),
             ],
             compiler_params=pltpu.CompilerParams(vmem_limit_bytes=65900000),
             name="scale",

time: 60.2 us -> 57.9 us (0.962)
  Pallas kernels: 58.1 us -> 56.3 us
    pallas_call x1, Pallas kernels: 55.5 us -> 54.4 us  [local(): pl.pallas_call(functools.partial(kernel, members, groups), out_shape=(jax...]
    pallas_call x1, Pallas kernels: 2.62 us -> 1.9 us  [local(): pl.pallas_call(functools.partial(scale_kernel, groups * total, total), ou...]
where the time goes in v6:
time: 57.9 us; the launch traced here: 57.6 us
  Pallas kernels  56.3 us (97%)
  between operations  1.29 us (2%)
    pallas_call x1, Pallas kernels, local(): pl.pallas_call(functools.partial(kernel, members, groups), out_shape=(jax...  54.4 us
    pallas_call x1, Pallas kernels, local(): pl.pallas_call(functools.partial(scale_kernel, groups * total, total), ou...  1.9 us

profile of v6, /device:TPU:1, one launch (start us, length us, event | category | flops | bytes accessed | tf_op | source)
XLA Modules:
  0.0 57.6 jit_solution(13117228001722006020)
XLA Ops:
  1.3 54.4 %sublayer.1 = (bf16[8,72,128]{2,1,0:T(8,128)(2,1)}, bf16[8,72,128]{2,1,0:T(8,128)(2,1)}, bf16[8,72,128]{2,1,0:T(8,128)(2,1)}, bf16[8,12,128]{2,1,0:T(8,128)(2,1)}, f32[32,1,128]{2,1,0:T(1,128)}) custom-call(s32[1]{0:T(128)S(6)} %copy.12.len_ref, s32[1,128]{1,0:T(1,128)} %seg_ref.1, bf16[8,72,128]{2,1,0:T(8,128)(2,1)} %bitcast.27, ...), custom_call_target="tpu_custom_call" | custom-call | tf_op jit(solution)/shard_map/sublayer/pallas_call | solution.py:623
  55.7 1.9 %scale.1 = (f32[576,128]{1,0:T(8,128)}, f32[576,128]{1,0:T(8,128)}, f32[576,128]{1,0:T(8,128)}, f32[36,36]{1,0:T(8,128)}, f32[1,1]{1,0:T(1,128)}) custom-call(f32[32,1,128]{2,1,0:T(1,128)} %get-tuple-element.15.sum_hbm, bf16[8,72,128]{2,1,0:T(8,128)(2,1)} %get-tuple-element.16.dq_hbm, bf16[8,72,128]{2,1,0:T(8,128)(2,1)} %get-tuple-element.17.dk_hbm, ...), custom_call_target="tpu_custom_call" | custom-call | tf_op jit(solution)/shard_map/scale/pallas_call | solution.py:705

commit v7 on v6

--- a/solution.py
+++ b/solution.py
@@ -62,6 +62,7 @@
     v_in,
     w_ref,
     t_ref,
+    len_row,
     seg_row,
     seg_all,
     q_slab,
@@ -130,7 +131,7 @@
     loads = [
         pltpu.make_async_copy(src, dst, load_sem.at[i])
         for i, (src, dst) in enumerate(
-            [(seg_ref, seg_row), (k_ref, k_in), (v_ref, v_in), (q_ref, q_in), (w_hbm, w_ref), (t_hbm, t_ref)]
+            [(seg_ref, seg_row), (k_ref, k_in), (v_ref, v_in), (q_ref, q_in), (w_hbm, w_ref), (t_hbm, t_ref), (len_ref, len_row)]
         )
     ]
     for load in loads:
@@ -139,7 +140,7 @@
     barrier = pltpu.get_barrier_semaphore()
     for shift in range(1, members):
         pl.semaphore_signal(barrier, inc=1, device_id=(dp, lax.rem(me + shift, members)), device_id_type=MESH)
-    for load in loads[:4]:
+    for load in loads[:4] + loads[6:]:
         load.wait()
     seg_all[0] = seg_row[...]
     leads = me == LEADER
@@ -203,7 +204,7 @@
             slot = chips - s
             copy(source.at[far(s)], slab.at[slot], send_sem.at[number], recv.at[group_of[slot]], peer_of(s)).start()
 
-    length = len_ref[0]
+    length = len_row[...]
     lane = lax.broadcasted_iota(jnp.int32, (1, rows), 1)
     sublane = lax.broadcasted_iota(jnp.int32, (16, rows), 0)
 
@@ -434,6 +435,7 @@
                 copy(sum_own, sum_all.at[groups - shift], send_sem.at[ALL_SUM], recv_sem.at[ALL_SUM], peer).start()
             local.append(pltpu.make_async_copy(sum_own, sum_all.at[0], load_sem.at[3]))
             local[-1].start()
+        if i == 1:
             arrived(xa_in, recv_sem.at[XA])
             summed = xa_ref[cx].astype(F32)
             for d in range(XS - 1):
@@ -629,7 +631,7 @@
                 jax.ShapeDtypeStruct((chips, FEAT // members // 3, LANES), BF16),
                 jax.ShapeDtypeStruct((groups, 1, LANES), F32),
             ),
-            in_specs=[pl.BlockSpec(memory_space=pltpu.SMEM)] + [hbm] * 6,
+            in_specs=[hbm] * 7,
             out_specs=(hbm,) * 5,
             scratch_shapes=[
                 bf(HEADS, *slab),
@@ -637,6 +639,7 @@
                 bf(HEADS, *slab),
                 bf(FEAT, WIDTH),
                 bf(rows, WIDTH),
+                pltpu.VMEM((1, 1), jnp.int32),
                 pltpu.VMEM((1, rows), jnp.int32),
                 pltpu.VMEM((members, 1, rows), jnp.int32),
                 bf(chips, *slab),
@@ -683,7 +686,7 @@
                 fl(members, 1, LANES),
                 fl(1, LANES),
                 pltpu.SemaphoreType.REGULAR,
-                dma((6,)),
+                dma((7,)),
                 dma((20,)),
                 dma((16,)),
                 dma((2 * len(PAIRS),)),
@@ -694,7 +697,7 @@
             compiler_params=pltpu.CompilerParams(collective_id=0, has_side_effects=True, vmem_limit_bytes=65900000),
             name="sublayer",
         )(
-            lengths,
+            lengths.reshape(1, 1),
             segments,
             heads(query_rows),
             heads(key_rows),

time: 57.9 us -> 57.6 us (level)
  no operation moved by 1% of the time
where the time goes in v7:
time: 57.6 us; the launch traced here: 57.4 us
  Pallas kernels  56.1 us (97%)
  between operations  1.29 us (2%)
    pallas_call x1, Pallas kernels, local(): pl.pallas_call(functools.partial(kernel, members, groups), out_shape=(jax...  54.2 us
    pallas_call x1, Pallas kernels, local(): pl.pallas_call(functools.partial(scale_kernel, groups * total, total), ou...  1.9 us

profile of v7, /device:TPU:1, one launch (start us, length us, event | category | flops | bytes accessed | tf_op | source)
XLA Modules:
  0.0 57.4 jit_solution(8659973891871501164)
XLA Ops:
  1.3 54.2 %sublayer.1 = (bf16[8,72,128]{2,1,0:T(8,128)(2,1)}, bf16[8,72,128]{2,1,0:T(8,128)(2,1)}, bf16[8,72,128]{2,1,0:T(8,128)(2,1)}, bf16[8,12,128]{2,1,0:T(8,128)(2,1)}, f32[32,1,128]{2,1,0:T(1,128)}) custom-call(s32[1,1]{1,0:T(1,128)} %bitcast.27.len_ref, s32[1,128]{1,0:T(1,128)} %seg_ref.1, bf16[8,72,128]{2,1,0:T(8,128)(2,1)} %bitcast.29, ...), custom_call_target="tpu_custom_call" | custom-call | tf_op jit(solution)/shard_map/sublayer/pallas_call | solution.py:625
  55.5 1.9 %scale.1 = (f32[576,128]{1,0:T(8,128)}, f32[576,128]{1,0:T(8,128)}, f32[576,128]{1,0:T(8,128)}, f32[36,36]{1,0:T(8,128)}, f32[1,1]{1,0:T(1,128)}) custom-call(f32[32,1,128]{2,1,0:T(1,128)} %get-tuple-element.15.sum_hbm, bf16[8,72,128]{2,1,0:T(8,128)(2,1)} %get-tuple-element.16.dq_hbm, bf16[8,72,128]{2,1,0:T(8,128)(2,1)} %get-tuple-element.17.dk_hbm, ...), custom_call_target="tpu_custom_call" | custom-call | tf_op jit(solution)/shard_map/scale/pallas_call | solution.py:708
